TPU v7x, 32 devices: a whole 2x2x4 slice. The times are simulated.
32 devices in a mesh: seq: 4 (over y, x), fsdp: 8 (over z, core).
Axes of the slice: x: 2, y: 2, z: 4, core: 2. Of those that a mesh axis runs over, the one named last changes fastest.
Arguments:
- audio_codes: int32 [8, 4, 1536], P('fsdp'), may hold values from 0 to 2047
- delay_masks: int32 [8, 4, 1536], P('fsdp'), may hold values from 0 to 1, as said below
- clip_lengths: int32 [8], P('fsdp'), may hold values from 768 to 1536, as said below
- text_states: bfloat16 [8, 64, 1024], P('fsdp'), may hold values from -6 to 6
- step_count: int32 [1], replicated, may hold values from 1 to 20
- attention_master: float32 [1, 8, 1024, 1024], P(None, None, ('seq', 'fsdp')), as said below
- attention_mean: float32 [1, 8, 1024, 1024], P(None, None, ('seq', 'fsdp')), may hold values from -5.722046e-06 to 5.722046e-06
- attention_square: float32 [1, 8, 1024, 1024], P(None, None, ('seq', 'fsdp')), may hold values from 8.6677144e-13 to 1.4446191e-11
- feedforward_master: float32 [1, 2, 1024, 4096], P(None, None, ('seq', 'fsdp')), may hold values from -0.1875 to 0.1875
- feedforward_mean: float32 [1, 2, 1024, 4096], P(None, None, ('seq', 'fsdp')), may hold values from -5.722046e-06 to 5.722046e-06
- feedforward_square: float32 [1, 2, 1024, 4096], P(None, None, ('seq', 'fsdp')), may hold values from 8.6677144e-13 to 1.4446191e-11
- tables_master: float32 [2, 4, 2048, 1024], P(None, None, ('seq', 'fsdp')), may hold values from -1 to 1, as said below
- tables_mean: float32 [2, 4, 2048, 1024], P(None, None, ('seq', 'fsdp')), may hold values from -5.722046e-06 to 5.722046e-06
- tables_square: float32 [2, 4, 2048, 1024], P(None, None, ('seq', 'fsdp')), may hold values from 8.6677144e-13 to 1.4446191e-11
- ahead_master: float32 [1024, 1024], P(('seq', 'fsdp')), may hold values from -0.1875 to 0.1875
- ahead_mean: float32 [1024, 1024], P(('seq', 'fsdp')), may hold values from -5.722046e-06 to 5.722046e-06
- ahead_square: float32 [1024, 1024], P(('seq', 'fsdp')), may hold values from 8.6677144e-13 to 1.4446191e-11
- norms_master: float32 [4, 2, 1024], P(None, None, ('seq', 'fsdp')), may hold values from -1 to 2, as said below
- norms_mean: float32 [4, 2, 1024], P(None, None, ('seq', 'fsdp')), may hold values from -5.722046e-06 to 5.722046e-06
- norms_square: float32 [4, 2, 1024], P(None, None, ('seq', 'fsdp')), may hold values from 8.6677144e-13 to 1.4446191e-11
Outputs:
- loss_value: float32 [], replicated
- gradient_norm: float32 [], replicated
- attention_master_new: float32 [1, 8, 1024, 1024], P(None, None, ('seq', 'fsdp'))
- attention_mean_new: float32 [1, 8, 1024, 1024], P(None, None, ('seq', 'fsdp'))
- attention_square_new: float32 [1, 8, 1024, 1024], P(None, None, ('seq', 'fsdp'))
- attention_rounded: bfloat16 [1, 8, 1024, 1024], P(None, None, ('seq', 'fsdp'))
- feedforward_master_new: float32 [1, 2, 1024, 4096], P(None, None, ('seq', 'fsdp'))
- feedforward_mean_new: float32 [1, 2, 1024, 4096], P(None, None, ('seq', 'fsdp'))
- feedforward_square_new: float32 [1, 2, 1024, 4096], P(None, None, ('seq', 'fsdp'))
- feedforward_rounded: bfloat16 [1, 2, 1024, 4096], P(None, None, ('seq', 'fsdp'))
- tables_master_new: float32 [2, 4, 2048, 1024], P(None, None, ('seq', 'fsdp'))
- tables_mean_new: float32 [2, 4, 2048, 1024], P(None, None, ('seq', 'fsdp'))
- tables_square_new: float32 [2, 4, 2048, 1024], P(None, None, ('seq', 'fsdp'))
- tables_rounded: bfloat16 [2, 4, 2048, 1024], P(None, None, ('seq', 'fsdp'))
- ahead_master_new: float32 [1024, 1024], P(('seq', 'fsdp'))
- ahead_mean_new: float32 [1024, 1024], P(('seq', 'fsdp'))
- ahead_square_new: float32 [1024, 1024], P(('seq', 'fsdp'))
- ahead_rounded: bfloat16 [1024, 1024], P(('seq', 'fsdp'))
- norms_master_new: float32 [4, 2, 1024], P(None, None, ('seq', 'fsdp'))
- norms_mean_new: float32 [4, 2, 1024], P(None, None, ('seq', 'fsdp'))
- norms_square_new: float32 [4, 2, 1024], P(None, None, ('seq', 'fsdp'))
- norms_rounded: bfloat16 [4, 2, 1024], P(None, None, ('seq', 'fsdp'))
Inputs may be any that keep to these rules, and one draw needn't show every extreme that they name: `delay_masks`: 1 where codebook k's id at a frame counts as a target; always 0 at frames before frame k of the delay pattern. `clip_lengths`: targets at frames at or beyond a clip's length don't count; the first clip is full. `attention_master`: normal entries, scaled per matrix. `norms_master`: gains between 0.6 and 1.4, biases between -0.4 and 0.4. `tables_master`: entries of deviation about 1/16.
All inputs are finite; a program needn't handle non-finite values.
Results may differ from a plain program's by a relative error of at most 0.0055.
The roundings to bfloat16 on the way count: a program that leaves them out, or rounds other values in their place, can miss the bound.
Values may be sent and summed in bfloat16 or wider, within the bound.
A program may use at most 320 MiB of HBM per device.

v0:
```python
from functools import partial
import math

import jax
import jax.numpy as jnp
from jax import lax
from jax.sharding import PartitionSpec as P

D = 1024
HD = 64
CODEBOOKS = 4
LAYERS = 1


norm_epsilon = 1e-05
first_decay = 0.9
second_decay = 0.95
learn_rate = 0.03
weight_decay = 0.1
adam_epsilon = 1e-08
clip_limit = 0.05
ahead_weight = 0.3
masked_score = -1e30


def combined_all(x, axis, combine):
    everything = jax.tree.map(lambda part: lax.all_gather(part, axis), x)
    first = jax.tree.map(lambda part: part[0], everything)

    def turn(k, so_far):
        return combine(so_far, jax.tree.map(lambda part: part[k], everything))

    return lax.fori_loop(1, lax.axis_size(axis), turn, first)


def float_dot(left, right):
    return jnp.dot(left, right, preferred_element_type=jnp.float32)


def dot_first(left, right):
    return lax.dot_general(
        left, right, (((0,), (0,)), ((), ())), preferred_element_type=jnp.float32
    )


def dot_last(left, right):
    return lax.dot_general(
        left, right, (((1,), (1,)), ((), ())), preferred_element_type=jnp.float32
    )


def layer_norm(residual, gain, bias):
    centered = residual - jnp.mean(residual, axis=-1, keepdims=True)
    variance = jnp.mean(centered * centered, axis=-1, keepdims=True)
    return centered * lax.rsqrt(variance + norm_epsilon) * gain + bias


def sinusoids(offset, row_count, width):
    half_width = width // 2
    log_rate = math.log(10000.0) / (half_width - 1)
    frequency = jnp.exp(jnp.arange(half_width, dtype=jnp.float32) * -log_rate)
    places = (offset + jnp.arange(row_count, dtype=jnp.float32))[:, None] * frequency[None, :]
    return jnp.concatenate([jnp.cos(places), jnp.sin(places)], axis=1)


def to_heads(blocks):
    return lax.all_to_all(blocks, "seq", split_axis=2, concat_axis=0, tiled=True)


def to_rows(blocks):
    return lax.all_to_all(blocks, "seq", split_axis=0, concat_axis=2, tiled=True)


def block_size():
    return 512


def causal_forward(queries, key_rows, value_rows):
    total_rows = queries.shape[0]
    block_rows = block_size()
    scale_factor = 1.0 / math.sqrt(queries.shape[2])
    outputs = []
    totals = []
    for block_index in range(total_rows // block_rows):
        start_row = block_index * block_rows
        stop_row = start_row + block_rows
        scores = (
            jnp.einsum(
                "qhd,khd->hqk",
                queries[start_row:stop_row],
                key_rows[:stop_row],
                preferred_element_type=jnp.float32,
            )
            * scale_factor
        )
        allowed = (start_row + jnp.arange(block_rows))[:, None] >= jnp.arange(stop_row)[None, :]
        scores = jnp.where(allowed[None], scores, masked_score)
        row_max = jnp.max(scores, axis=2, keepdims=True)
        exponent = jnp.exp(scores - row_max)
        row_sum = jnp.sum(exponent, axis=2, keepdims=True)
        probs_low = (exponent / row_sum).astype(jnp.bfloat16)
        outputs.append(
            jnp.einsum(
                "hqk,khd->qhd", probs_low, value_rows[:stop_row], preferred_element_type=jnp.float32
            )
        )
        totals.append(row_max + jnp.log(row_sum))
    return (jnp.concatenate(outputs, axis=0), jnp.concatenate(totals, axis=1))


def causal_backward(queries, key_rows, value_rows, log_totals, grad_out):
    total_rows = queries.shape[0]
    block_rows = block_size()
    scale_factor = 1.0 / math.sqrt(queries.shape[2])
    grad_queries = []
    grad_keys = jnp.zeros(key_rows.shape, jnp.float32)
    grad_values = jnp.zeros(value_rows.shape, jnp.float32)
    for block_index in range(total_rows // block_rows):
        start_row = block_index * block_rows
        stop_row = start_row + block_rows
        query_part = queries[start_row:stop_row]
        out_part = grad_out[start_row:stop_row]
        scores = (
            jnp.einsum(
                "qhd,khd->hqk", query_part, key_rows[:stop_row], preferred_element_type=jnp.float32
            )
            * scale_factor
        )
        allowed = (start_row + jnp.arange(block_rows))[:, None] >= jnp.arange(stop_row)[None, :]
        scores = jnp.where(allowed[None], scores, masked_score)
        attention_probs = jnp.exp(scores - log_totals[:, start_row:stop_row])
        probs_low = attention_probs.astype(jnp.bfloat16)
        grad_probs = jnp.einsum(
            "qhd,khd->hqk", out_part, value_rows[:stop_row], preferred_element_type=jnp.float32
        )
        grad_scores = attention_probs * (
            grad_probs - jnp.sum(attention_probs * grad_probs, axis=2, keepdims=True)
        )
        scores_low = grad_scores.astype(jnp.bfloat16)
        grad_queries.append(
            scale_factor
            * jnp.einsum(
                "hqk,khd->qhd", scores_low, key_rows[:stop_row], preferred_element_type=jnp.float32
            )
        )
        grad_keys = grad_keys.at[:stop_row].add(
            scale_factor
            * jnp.einsum("hqk,qhd->khd", scores_low, query_part, preferred_element_type=jnp.float32)
        )
        grad_values = grad_values.at[:stop_row].add(
            jnp.einsum("hqk,qhd->khd", probs_low, out_part, preferred_element_type=jnp.float32)
        )
    return (jnp.concatenate(grad_queries, axis=0), grad_keys, grad_values)


def cross_forward(queries, key_rows, value_rows):
    scale_factor = 1.0 / math.sqrt(queries.shape[2])
    scores = (
        jnp.einsum("qhd,khd->hqk", queries, key_rows, preferred_element_type=jnp.float32)
        * scale_factor
    )
    row_max = jnp.max(scores, axis=2, keepdims=True)
    exponent = jnp.exp(scores - row_max)
    row_sum = jnp.sum(exponent, axis=2, keepdims=True)
    probs_low = (exponent / row_sum).astype(jnp.bfloat16)
    output = jnp.einsum("hqk,khd->qhd", probs_low, value_rows, preferred_element_type=jnp.float32)
    return (output, row_max + jnp.log(row_sum))


def cross_backward(queries, key_rows, value_rows, log_totals, grad_out):
    scale_factor = 1.0 / math.sqrt(queries.shape[2])
    scores = (
        jnp.einsum("qhd,khd->hqk", queries, key_rows, preferred_element_type=jnp.float32)
        * scale_factor
    )
    attention_probs = jnp.exp(scores - log_totals)
    probs_low = attention_probs.astype(jnp.bfloat16)
    grad_probs = jnp.einsum(
        "qhd,khd->hqk", grad_out, value_rows, preferred_element_type=jnp.float32
    )
    grad_scores = attention_probs * (
        grad_probs - jnp.sum(attention_probs * grad_probs, axis=2, keepdims=True)
    )
    scores_low = grad_scores.astype(jnp.bfloat16)
    grad_queries = scale_factor * jnp.einsum(
        "hqk,khd->qhd", scores_low, key_rows, preferred_element_type=jnp.float32
    )
    grad_keys = scale_factor * jnp.einsum(
        "hqk,qhd->khd", scores_low, queries, preferred_element_type=jnp.float32
    )
    grad_values = jnp.einsum(
        "hqk,qhd->khd", probs_low, grad_out, preferred_element_type=jnp.float32
    )
    return (grad_queries, grad_keys, grad_values)


def layer_forward(residual, gathered, text_clip, seq_index, seq_count):
    matrices, feedforward_w, norm_params = gathered
    norm_float = norm_params.astype(jnp.float32)
    head_width = matrices.shape[2] // seq_count
    heads_here = head_width // HD
    text_rows = text_clip.shape[0]
    normed_self = layer_norm(residual, norm_float[0, 0], norm_float[0, 1]).astype(jnp.bfloat16)
    projected = jnp.einsum(
        "rd,jde->rje", normed_self, matrices[0:3], preferred_element_type=jnp.float32
    )
    heads_qkv = to_heads(projected.astype(jnp.bfloat16))
    total_rows = heads_qkv.shape[0]
    queries = heads_qkv[:, 0].reshape(total_rows, heads_here, HD)
    key_rows = heads_qkv[:, 1].reshape(total_rows, heads_here, HD)
    value_rows = heads_qkv[:, 2].reshape(total_rows, heads_here, HD)
    attended, self_totals = causal_forward(queries, key_rows, value_rows)
    self_rows = to_rows(attended.astype(jnp.bfloat16).reshape(total_rows, 1, head_width))[:, 0]
    after_self = residual + float_dot(self_rows, matrices[3])
    normed_cross = layer_norm(after_self, norm_float[1, 0], norm_float[1, 1]).astype(jnp.bfloat16)
    cross_query = float_dot(normed_cross, matrices[4]).astype(jnp.bfloat16)
    cross_heads = to_heads(cross_query[:, None, :])[:, 0].reshape(total_rows, heads_here, HD)
    column_start = seq_index * head_width
    key_columns = lax.dynamic_slice_in_dim(matrices[5], column_start, head_width, 1)
    value_columns = lax.dynamic_slice_in_dim(matrices[6], column_start, head_width, 1)
    cross_keys = (
        float_dot(text_clip, key_columns).astype(jnp.bfloat16).reshape(text_rows, heads_here, HD)
    )
    cross_values = (
        float_dot(text_clip, value_columns).astype(jnp.bfloat16).reshape(text_rows, heads_here, HD)
    )
    cross_out, cross_totals = cross_forward(cross_heads, cross_keys, cross_values)
    cross_rows = to_rows(cross_out.astype(jnp.bfloat16).reshape(total_rows, 1, head_width))[:, 0]
    after_cross = after_self + float_dot(cross_rows, matrices[7])
    normed_feed = layer_norm(after_cross, norm_float[2, 0], norm_float[2, 1]).astype(jnp.bfloat16)
    hidden_pre = float_dot(normed_feed, feedforward_w[0])
    hidden_low = jax.nn.gelu(hidden_pre, approximate=False).astype(jnp.bfloat16)
    output = after_cross + dot_last(hidden_low, feedforward_w[1])
    saved = (
        normed_self,
        queries,
        key_rows,
        value_rows,
        self_totals,
        self_rows,
        after_self,
        normed_cross,
        cross_heads,
        cross_keys,
        cross_values,
        cross_totals,
        cross_rows,
        after_cross,
        normed_feed,
        hidden_pre,
        hidden_low,
    )
    return (output, saved)


def layer_backward(residual, gathered, text_clip, saved, grad_residual, seq_index, seq_count):
    matrices, feedforward_w, norm_params = gathered
    norm_float = norm_params.astype(jnp.float32)
    (
        normed_self,
        queries,
        key_rows,
        value_rows,
        self_totals,
        self_rows,
        after_self,
        normed_cross,
        cross_heads,
        cross_keys,
        cross_values,
        cross_totals,
        cross_rows,
        after_cross,
        normed_feed,
        hidden_pre,
        hidden_low,
    ) = saved
    head_width = matrices.shape[2] // seq_count
    heads_here = head_width // HD
    total_rows = queries.shape[0]
    text_rows = text_clip.shape[0]
    column_start = seq_index * head_width
    branch_low = grad_residual.astype(jnp.bfloat16)
    grad_down = dot_first(branch_low, hidden_low)
    grad_hidden = float_dot(branch_low, feedforward_w[1])
    unused_gelu, gelu_pull = jax.vjp(partial(jax.nn.gelu, approximate=False), hidden_pre)
    grad_pre = gelu_pull(grad_hidden)[0].astype(jnp.bfloat16)
    grad_up = dot_first(normed_feed, grad_pre)
    grad_normed = dot_last(grad_pre, feedforward_w[0])
    unused_norm, norm_pull = jax.vjp(layer_norm, after_cross, norm_float[2, 0], norm_float[2, 1])
    grad_inner, feed_gain, feed_bias = norm_pull(grad_normed)
    grad_residual = grad_residual + grad_inner
    branch_low = grad_residual.astype(jnp.bfloat16)
    grad_cross_out = dot_first(cross_rows, branch_low)
    grad_rows = dot_last(branch_low, matrices[7]).astype(jnp.bfloat16)
    grad_heads = to_heads(grad_rows[:, None, :])[:, 0].reshape(total_rows, heads_here, HD)
    grad_cq, grad_ck, grad_cv = cross_backward(
        cross_heads, cross_keys, cross_values, cross_totals, grad_heads
    )
    grad_cq_rows = to_rows(grad_cq.astype(jnp.bfloat16).reshape(total_rows, 1, head_width))[:, 0]
    grad_cross_query = dot_first(normed_cross, grad_cq_rows)
    grad_normed = dot_last(grad_cq_rows, matrices[4])
    key_low = grad_ck.reshape(text_rows, head_width).astype(jnp.bfloat16)
    value_low = grad_cv.reshape(text_rows, head_width).astype(jnp.bfloat16)
    zero_matrix = jnp.zeros((matrices.shape[1], matrices.shape[2]), jnp.float32)
    grad_cross_keys = lax.dynamic_update_slice_in_dim(
        zero_matrix, dot_first(text_clip, key_low), column_start, 1
    )
    grad_cross_values = lax.dynamic_update_slice_in_dim(
        zero_matrix, dot_first(text_clip, value_low), column_start, 1
    )
    unused_norm, norm_pull = jax.vjp(layer_norm, after_self, norm_float[1, 0], norm_float[1, 1])
    grad_inner, cross_gain, cross_bias = norm_pull(grad_normed)
    grad_residual = grad_residual + grad_inner
    branch_low = grad_residual.astype(jnp.bfloat16)
    grad_self_out = dot_first(self_rows, branch_low)
    grad_rows = dot_last(branch_low, matrices[3]).astype(jnp.bfloat16)
    grad_heads = to_heads(grad_rows[:, None, :])[:, 0].reshape(total_rows, heads_here, HD)
    grad_q, grad_k, grad_v = causal_backward(queries, key_rows, value_rows, self_totals, grad_heads)
    stacked = (
        jnp.stack([grad_q, grad_k, grad_v], axis=1)
        .reshape(total_rows, 3, head_width)
        .astype(jnp.bfloat16)
    )
    grad_qkv_rows = to_rows(stacked)
    grad_qkv = jnp.einsum(
        "rd,rje->jde", normed_self, grad_qkv_rows, preferred_element_type=jnp.float32
    )
    grad_normed = jnp.einsum(
        "rje,jde->rd", grad_qkv_rows, matrices[0:3], preferred_element_type=jnp.float32
    )
    unused_norm, norm_pull = jax.vjp(layer_norm, residual, norm_float[0, 0], norm_float[0, 1])
    grad_inner, self_gain, self_bias = norm_pull(grad_normed)
    grad_residual = grad_residual + grad_inner
    grad_matrices = jnp.concatenate(
        [
            grad_qkv,
            grad_self_out[None],
            grad_cross_query[None],
            grad_cross_keys[None],
            grad_cross_values[None],
            grad_cross_out[None],
        ],
        axis=0,
    )
    grad_feed = jnp.stack([grad_up, grad_down], axis=0)
    grad_norms = jnp.stack(
        [
            jnp.stack([self_gain, self_bias]),
            jnp.stack([cross_gain, cross_bias]),
            jnp.stack([feed_gain, feed_bias]),
        ],
        axis=0,
    )
    return (grad_residual, grad_matrices, grad_feed, grad_norms)


def combine_stats(first, second):
    first_max, first_sum, first_pick = first
    second_max, second_sum, second_pick = second
    joint_max = jnp.maximum(first_max, second_max)
    joint_sum = first_sum * jnp.exp(first_max - joint_max) + second_sum * jnp.exp(
        second_max - joint_max
    )
    return (joint_max, joint_sum, first_pick + second_pick)


def adamw_update(master, mean, square, gradient, factor, first_fix, second_fix, decay):
    gradient = gradient * factor
    mean_new = first_decay * mean + (1.0 - first_decay) * gradient
    square_new = second_decay * square + (1.0 - second_decay) * gradient * gradient
    change = learn_rate * (
        mean_new / first_fix / (jnp.sqrt(square_new / second_fix) + adam_epsilon) + decay * master
    )
    master_new = master - change
    return (master_new, mean_new, square_new, master_new.astype(jnp.bfloat16))


def on_device(
    audio_codes,
    delay_masks,
    clip_lengths,
    text_states,
    step_count,
    attention_master,
    attention_mean,
    attention_square,
    feedforward_master,
    feedforward_mean,
    feedforward_square,
    tables_master,
    tables_mean,
    tables_square,
    ahead_master,
    ahead_mean,
    ahead_square,
    norms_master,
    norms_mean,
    norms_square,
):
    seq_count = lax.axis_size("seq")
    seq_index = lax.axis_index("seq")
    clips_total = lax.axis_size("fsdp")
    codes_clip = audio_codes[0]
    masks_clip = delay_masks[0]
    length_clip = clip_lengths[0]
    text_clip = text_states[0]
    total_rows = codes_clip.shape[1]
    rows_here = total_rows // seq_count
    row_start = seq_index * rows_here
    scale_norm = 1.0 / (CODEBOOKS * total_rows * clips_total)
    attention_low = attention_master.astype(jnp.bfloat16)
    feedforward_low = feedforward_master.astype(jnp.bfloat16)
    tables_low = tables_master.astype(jnp.bfloat16)
    ahead_low = ahead_master.astype(jnp.bfloat16)
    norms_low = norms_master.astype(jnp.bfloat16)
    attention_all, feedforward_all, norms_all, ahead_full = (
        lax.all_gather(attention_low, ("seq", "fsdp"), axis=2, tiled=True),
        lax.all_gather(feedforward_low, ("seq", "fsdp"), axis=2, tiled=True),
        lax.all_gather(norms_low, ("seq", "fsdp"), axis=2, tiled=True),
        lax.all_gather(ahead_low, ("seq", "fsdp"), axis=0, tiled=True),
    )
    tables_part = lax.all_gather(tables_low, "fsdp", axis=2, tiled=True)
    final_norm = norms_all[3 * LAYERS]
    vocab_part = tables_part.shape[2]
    vocab_start = seq_index * vocab_part
    vocab_range = jnp.arange(vocab_part, dtype=jnp.int32)
    local_ids = codes_clip - vocab_start
    inside = (local_ids >= 0) & (local_ids < vocab_part)
    safe_ids = jnp.where(inside, local_ids, 0)
    embed_sum = jnp.zeros((total_rows, D), jnp.float32)
    for codebook in range(CODEBOOKS):
        looked = jnp.take(tables_part[0, codebook], safe_ids[codebook], axis=0).astype(jnp.float32)
        embed_sum = embed_sum + jnp.where(inside[codebook][:, None], looked, 0.0)
    embedded = lax.psum_scatter(embed_sum, "seq", scatter_dimension=0, tiled=True)
    residual = embedded + sinusoids(row_start.astype(jnp.float32), rows_here, D)

    def layer_of(layer_index):
        return (
            attention_all[layer_index],
            feedforward_all[layer_index],
            norms_all[3 * layer_index : 3 * layer_index + 3],
        )

    layer_index = 0
    layer_inputs = [residual]
    residual, unused_saved = layer_forward(
        residual, layer_of(layer_index), text_clip, seq_index, seq_count
    )
    final_float = final_norm.astype(jnp.float32)
    final_low = layer_norm(residual, final_float[0], final_float[1]).astype(jnp.bfloat16)
    ahead_rows = float_dot(final_low, ahead_full).astype(jnp.bfloat16)
    final_all, ahead_all = (
        lax.all_gather(final_low, "seq", axis=0, tiled=True),
        lax.all_gather(ahead_rows, "seq", axis=0, tiled=True),
    )
    frames = jnp.arange(total_rows, dtype=jnp.int32)
    target_sets = []
    for target_shift in (1, 2):
        padding = jnp.zeros((CODEBOOKS, target_shift), jnp.int32)
        targets = jnp.concatenate([codes_clip[:, target_shift:], padding], axis=1)
        live_mask = jnp.concatenate([masks_clip[:, target_shift:], padding], axis=1)
        live_mask = live_mask * (frames + target_shift < length_clip).astype(jnp.int32)
        local_targets = targets - vocab_start
        target_inside = (local_targets >= 0) & (local_targets < vocab_part)
        safe_targets = jnp.where(target_inside, local_targets, 0)
        target_sets.append((safe_targets, target_inside, live_mask.astype(jnp.float32)))
    sources = (final_all, ahead_all)
    logit_blocks = []
    maxima = []
    sums = []
    picks = []
    for objective_index in range(2):
        safe_targets, target_inside, live_mask = target_sets[objective_index]
        for codebook in range(CODEBOOKS):
            logits = dot_last(sources[objective_index], tables_part[1, codebook])
            row_max = jnp.max(logits, axis=1)
            row_sum = jnp.sum(jnp.exp(logits - row_max[:, None]), axis=1)
            picked = jnp.take_along_axis(logits, safe_targets[codebook][:, None], axis=1)[:, 0]
            logit_blocks.append(logits)
            maxima.append(row_max)
            sums.append(row_sum)
            picks.append(jnp.where(target_inside[codebook], picked, 0.0))
    merged_max, merged_sum, merged_pick = combined_all(
        (jnp.stack(maxima), jnp.stack(sums), jnp.stack(picks)), "seq", combine_stats
    )
    log_totals = merged_max + jnp.log(merged_sum)
    factors = jnp.array([1.0] * CODEBOOKS + [ahead_weight] * CODEBOOKS, jnp.float32)[:, None]
    weighted = factors * jnp.concatenate([target_sets[0][2], target_sets[1][2]], axis=0)
    own_terms = lax.dynamic_slice_in_dim(
        weighted * (log_totals - merged_pick), row_start, rows_here, 1
    )
    own_loss = jnp.sum(own_terms)
    grad_final_part = jnp.zeros((total_rows, D), jnp.float32)
    grad_ahead_part = jnp.zeros((total_rows, D), jnp.float32)
    head_grads = [jnp.zeros((vocab_part, D), jnp.float32) for codebook in range(CODEBOOKS)]
    for objective_index in range(2):
        safe_targets, target_inside, live_mask = target_sets[objective_index]
        for codebook in range(CODEBOOKS):
            position = objective_index * CODEBOOKS + codebook
            attention_probs = jnp.exp(logit_blocks[position] - log_totals[position][:, None])
            onehot = (
                (vocab_range[None, :] == safe_targets[codebook][:, None])
                & target_inside[codebook][:, None]
            ).astype(jnp.float32)
            coefficient = (weighted[position] * scale_norm)[:, None]
            grad_low = (coefficient * (attention_probs - onehot)).astype(jnp.bfloat16)
            part_rows = float_dot(grad_low, tables_part[1, codebook])
            if objective_index == 0:
                grad_final_part = grad_final_part + part_rows
            else:
                grad_ahead_part = grad_ahead_part + part_rows
            head_grads[codebook] = head_grads[codebook] + dot_first(
                grad_low, sources[objective_index]
            )
    grad_final_rows, grad_ahead_rows = (
        lax.psum_scatter(grad_final_part, "seq", scatter_dimension=0, tiled=True),
        lax.psum_scatter(grad_ahead_part, "seq", scatter_dimension=0, tiled=True),
    )
    ahead_grad_low = grad_ahead_rows.astype(jnp.bfloat16)
    grad_ahead_matrix = dot_first(final_low, ahead_grad_low)
    grad_final = grad_final_rows + dot_last(ahead_grad_low, ahead_full)
    unused_norm, final_pull = jax.vjp(layer_norm, residual, final_float[0], final_float[1])
    grad_residual, final_gain, final_bias = final_pull(grad_final)
    matrix_grads = [None] * LAYERS
    feed_grads = [None] * LAYERS
    norm_grads = [None] * LAYERS
    for layer_index in reversed(range(LAYERS)):
        gathered = layer_of(layer_index)
        unused_output, saved = layer_forward(
            layer_inputs[layer_index], gathered, text_clip, seq_index, seq_count
        )
        grad_residual, grad_matrices, grad_feed, grad_norms = layer_backward(
            layer_inputs[layer_index],
            gathered,
            text_clip,
            saved,
            grad_residual,
            seq_index,
            seq_count,
        )
        matrix_grads[layer_index] = grad_matrices
        feed_grads[layer_index] = grad_feed
        norm_grads[layer_index] = grad_norms
    embed_grad_low = grad_residual.astype(jnp.bfloat16)
    embed_grad_all = lax.all_gather(embed_grad_low, "seq", axis=0, tiled=True)
    embed_grads = []
    for codebook in range(CODEBOOKS):
        onehot_ids = (
            (safe_ids[codebook][:, None] == vocab_range[None, :]) & inside[codebook][:, None]
        ).astype(jnp.bfloat16)
        embed_grads.append(dot_first(onehot_ids, embed_grad_all))
    grad_tables = jnp.stack([jnp.stack(embed_grads), jnp.stack(head_grads)])
    attention_local = jnp.stack(matrix_grads)
    feedforward_local = jnp.stack(feed_grads)
    norms_local = jnp.concatenate(norm_grads + [jnp.stack([final_gain, final_bias])[None]], axis=0)
    attention_grad, feedforward_grad, norms_grad, ahead_grad_shard = (
        lax.psum_scatter(attention_local, ("seq", "fsdp"), scatter_dimension=2, tiled=True),
        lax.psum_scatter(feedforward_local, ("seq", "fsdp"), scatter_dimension=2, tiled=True),
        lax.psum_scatter(norms_local, ("seq", "fsdp"), scatter_dimension=2, tiled=True),
        lax.psum_scatter(grad_ahead_matrix, ("seq", "fsdp"), scatter_dimension=0, tiled=True),
    )
    tables_grad_shard = lax.psum_scatter(grad_tables, "fsdp", scatter_dimension=2, tiled=True)
    squares = (
        jnp.sum(attention_grad * attention_grad)
        + jnp.sum(feedforward_grad * feedforward_grad)
        + jnp.sum(tables_grad_shard * tables_grad_shard)
        + jnp.sum(ahead_grad_shard * ahead_grad_shard)
        + jnp.sum(norms_grad * norms_grad)
    )
    total_squares, total_loss = lax.psum((squares, own_loss), ("seq", "fsdp"))
    gradient_norm = jnp.sqrt(total_squares)
    loss_value = total_loss * scale_norm
    factor = jnp.minimum(1.0, clip_limit / (gradient_norm + 1e-06))
    step_value = step_count[0].astype(jnp.float32)
    first_fix = 1.0 - jnp.power(first_decay, step_value)
    second_fix = 1.0 - jnp.power(second_decay, step_value)
    attention_new = adamw_update(
        attention_master,
        attention_mean,
        attention_square,
        attention_grad,
        factor,
        first_fix,
        second_fix,
        weight_decay,
    )
    feedforward_new = adamw_update(
        feedforward_master,
        feedforward_mean,
        feedforward_square,
        feedforward_grad,
        factor,
        first_fix,
        second_fix,
        weight_decay,
    )
    tables_new = adamw_update(
        tables_master,
        tables_mean,
        tables_square,
        tables_grad_shard,
        factor,
        first_fix,
        second_fix,
        weight_decay,
    )
    ahead_new = adamw_update(
        ahead_master,
        ahead_mean,
        ahead_square,
        ahead_grad_shard,
        factor,
        first_fix,
        second_fix,
        weight_decay,
    )
    norms_new = adamw_update(
        norms_master, norms_mean, norms_square, norms_grad, factor, first_fix, second_fix, 0.0
    )
    return (
        loss_value,
        gradient_norm,
        attention_new[0],
        attention_new[1],
        attention_new[2],
        attention_new[3],
        feedforward_new[0],
        feedforward_new[1],
        feedforward_new[2],
        feedforward_new[3],
        tables_new[0],
        tables_new[1],
        tables_new[2],
        tables_new[3],
        ahead_new[0],
        ahead_new[1],
        ahead_new[2],
        ahead_new[3],
        norms_new[0],
        norms_new[1],
        norms_new[2],
        norms_new[3],
    )


def solution(mesh):
    placed = (
        P("fsdp", None, None),
        P("fsdp", None, None),
        P("fsdp"),
        P("fsdp", None, None),
        P(),
        P(None, None, ("seq", "fsdp"), None),
        P(None, None, ("seq", "fsdp"), None),
        P(None, None, ("seq", "fsdp"), None),
        P(None, None, ("seq", "fsdp"), None),
        P(None, None, ("seq", "fsdp"), None),
        P(None, None, ("seq", "fsdp"), None),
        P(None, None, ("seq", "fsdp"), None),
        P(None, None, ("seq", "fsdp"), None),
        P(None, None, ("seq", "fsdp"), None),
        P(("seq", "fsdp"), None),
        P(("seq", "fsdp"), None),
        P(("seq", "fsdp"), None),
        P(None, None, ("seq", "fsdp")),
        P(None, None, ("seq", "fsdp")),
        P(None, None, ("seq", "fsdp")),
    )
    return jax.shard_map(
        on_device,
        mesh=mesh,
        in_specs=placed,
        out_specs=(
            P(),
            P(),
            P(None, None, ("seq", "fsdp"), None),
            P(None, None, ("seq", "fsdp"), None),
            P(None, None, ("seq", "fsdp"), None),
            P(None, None, ("seq", "fsdp"), None),
            P(None, None, ("seq", "fsdp"), None),
            P(None, None, ("seq", "fsdp"), None),
            P(None, None, ("seq", "fsdp"), None),
            P(None, None, ("seq", "fsdp"), None),
            P(None, None, ("seq", "fsdp"), None),
            P(None, None, ("seq", "fsdp"), None),
            P(None, None, ("seq", "fsdp"), None),
            P(None, None, ("seq", "fsdp"), None),
            P(("seq", "fsdp"), None),
            P(("seq", "fsdp"), None),
            P(("seq", "fsdp"), None),
            P(("seq", "fsdp"), None),
            P(None, None, ("seq", "fsdp")),
            P(None, None, ("seq", "fsdp")),
            P(None, None, ("seq", "fsdp")),
            P(None, None, ("seq", "fsdp")),
        ),
        check_vma=False,
    )
```

profile of v0, /device:TPU:12, one launch (start us, length us, event | category | flops | bytes accessed | tf_op | source)
XLA Modules:
  0.0 2807.2 jit_solution(1336441827695747588)
XLA Ops:
  12.3 79.4 %all-gather.11.cloned.1.call-done = bf16[2,4,512,1024]{3,2,1,0:T(8,128)(2,1)} async-done(((bf16[2,4,64,1024]{3,2,1,0:T(8,128)(2,1)}), bf16[2,4,512,1024]{3,2,1,0:T(8,128)(2,1)}) %all-gather.11.cloned.1.call-update) | async-done | bytes 8388624 | tf_op jit(solution)/shard_map/all_gather | solution.py:423
  122.2 10.7 select_add_fusion
  136.1 43.1 %all_gather.43 = bf16[4,2,1024]{0,1,2:T(2,128)(2,1)S(1)} all-gather(bf16[4,2,32]{0,1,2:T(2,128)(2,1)S(1)} %copy.246), channel_id=1, replica_groups=mesh['seq'=4,'fsdp'=8] {'seq','fsdp'}, dimensions={2}, use_global_device_ids=true | all-gather | bytes 16896 | tf_op jit(solution)/shard_map/all_gather | solution.py:420
  183.1 17.1 slice_reduce_fusion.3
  200.2 18.4 reduce-scatter.11.cloned.1.call-done
  220.7 46.4 %all-gather.13.cloned.1.call-done = bf16[1,8,1024,1024]{3,2,1,0:T(8,128)(2,1)} async-done(((bf16[1,8,32,1024]{3,2,1,0:T(8,128)(2,1)}), bf16[1,8,1024,1024]{3,2,1,0:T(8,128)(2,1)}) %all-gather.13.cloned.1.call-update) | async-done | bytes 16777232 | tf_op jit(solution)/shard_map/all_gather | solution.py:418
  288.8 47.9 %all-to-all-done = bf16[384,3,1024]{0,1,2:T(4,128)(2,1)} async-done(((bf16[384,3,1024]{0,1,2:T(4,128)(2,1)}), bf16[384,3,1024]{0,1,2:T(4,128)(2,1)}, u32[]{:S(2)}, u32[]{:S(2)}) %all-to-all-start) | async-done | bytes 2359328 | tf_op jit(solution)/shard_map/all_to_all | solution.py:67
  406.9 10.1 all-to-all-done.1
  492.2 20.0 multiply_convert_fusion.2
  539.5 39.3 %all-gather.17.cloned.1.call-done = bf16[1536,1024]{1,0:T(8,128)(2,1)} async-done(((bf16[384,1024]{1,0:T(8,128)(2,1)}), bf16[1536,1024]{1,0:T(8,128)(2,1)}) %all-gather.17.cloned.1.call-update) | async-done | bytes 3145744 | tf_op jit(solution)/shard_map/all_gather | solution.py:454
  600.7 24.3 all-gather.21.cloned.1.call-done
  675.9 55.8 %gather_fusion.7 = f32[1536]{0:T(1024)S(1)} fusion(f32[1536,512]{0,1:T(8,128)} %get-tuple-element.599, s32[1536]{0:T(1024)S(1)} %fusion.231), kind=kCustom, calls=%fused_computation.7.clone | custom fusion | bytes 24576 | tf_op jit(solution)/shard_map/jit(take_along_axis)/gather | solution.py:479
  731.8 61.1 %gather_fusion.6 = f32[1536]{0:T(1024)} fusion(f32[1536,512]{0,1:T(8,128)} %get-tuple-element.597, s32[1536]{0:T(1024)S(1)} %fusion.230), kind=kCustom, calls=%fused_computation.6.clone | custom fusion | bytes 24576 | tf_op jit(solution)/shard_map/jit(take_along_axis)/gather | solution.py:479
  792.9 61.4 %gather_fusion.5 = f32[1536]{0:T(1024)} fusion(f32[1536,512]{0,1:T(8,128)} %get-tuple-element.595, s32[1536]{0:T(1024)S(1)} %fusion.229), kind=kCustom, calls=%fused_computation.5.clone | custom fusion | bytes 24576 | tf_op jit(solution)/shard_map/jit(take_along_axis)/gather | solution.py:479
  854.4 62.1 %gather_fusion.4 = f32[1536]{0:T(1024)} fusion(f32[1536,512]{0,1:T(8,128)} %get-tuple-element.593, s32[1536]{0:T(1024)S(1)} %fusion.228), kind=kCustom, calls=%fused_computation.1.clone | custom fusion | bytes 24576 | tf_op jit(solution)/shard_map/jit(take_along_axis)/gather | solution.py:479
  916.5 12.7 gather_fusion.11
  929.2 54.7 %gather_fusion.10 = f32[1536]{0:T(1024)S(1)} fusion(f32[1536,512]{0,1:T(8,128)} %get-tuple-element.605, s32[1536]{0:T(1024)S(1)} %fusion.234), kind=kCustom, calls=%fused_computation.10.clone | custom fusion | bytes 24576 | tf_op jit(solution)/shard_map/jit(take_along_axis)/gather | solution.py:479
  983.9 55.0 %gather_fusion.9 = f32[1536]{0:T(1024)S(1)} fusion(f32[1536,512]{0,1:T(8,128)} %get-tuple-element.603, s32[1536]{0:T(1024)S(1)} %fusion.233), kind=kCustom, calls=%fused_computation.9.clone | custom fusion | bytes 24576 | tf_op jit(solution)/shard_map/jit(take_along_axis)/gather | solution.py:479
  1038.9 55.9 %gather_fusion.8 = f32[1536]{0:T(1024)S(1)} fusion(f32[1536,512]{0,1:T(8,128)} %get-tuple-element.601, s32[1536]{0:T(1024)S(1)} %fusion.232), kind=kCustom, calls=%fused_computation.8.clone | custom fusion | bytes 24576 | tf_op jit(solution)/shard_map/jit(take_along_axis)/gather | solution.py:479
  1151.9 52.6 %reduce-scatter.13.cloned.1.call-done = f32[384,1024]{1,0:T(8,128)} async-done(((f32[1536,1024]{1,0:T(8,128)}), f32[384,1024]{1,0:T(8,128)}) %reduce-scatter.13.cloned.1.call-update) | async-done | bytes 1572880 | tf_op jit(solution)/shard_map/reduce_scatter | solution.py:517
  1204.5 72.9 %reduce-scatter.15.cloned.1.call-done = f32[384,1024]{1,0:T(8,128)} async-done(((f32[1536,1024]{1,0:T(8,128)}), f32[384,1024]{1,0:T(8,128)}) %reduce-scatter.15.cloned.1.call-update) | async-done | bytes 1572880 | tf_op jit(solution)/shard_map/reduce_scatter | solution.py:518
  1283.2 12.0 add_convert_fusion
  1328.0 10.4 all-to-all-done.4
  1364.3 9.9 all-to-all-done.5
  1502.8 38.9 %all_to_all.146 = bf16[1536,3,256]{2,1,0:T(4,128)(2,1)} all-to-all(bf16[1536,3,256]{2,1,0:T(4,128)(2,1)S(1)} %pad_maximum_fusion.1), channel_id=1, replica_groups=mesh['seq'=4,'fsdp'=8] {'seq'}, dimensions={0} | all-to-all | bytes 4718592 | tf_op jit(solution)/shard_map/all_to_all | solution.py:71
  1634.8 11.3 maximum_bitcast_fusion
  1673.0 33.1 %copy.288 = f32[1,8,1024,1024]{3,1,0,2:T(8,128)} copy(f32[1,8,1024,1024]{2,3,1,0:T(8,128)} %bitcast.122) | data formatting | bytes 67108864 | tf_op jit(solution)/shard_map/stack | solution.py:554
  1710.0 125.1 %reduce-scatter.23.cloned.1.call-done = f32[32,1024]{1,0:T(8,128)} async-done(((f32[1024,1024]{1,0:T(8,128)}), f32[32,1024]{1,0:T(8,128)}) %reduce-scatter.23.cloned.1.call-update) | async-done | bytes 131088 | tf_op jit(solution)/shard_map/reduce_scatter | solution.py:561
  1836.6 169.3 %reduce-scatter.21.cloned.1.call-done = f32[2,4,64,1024]{3,2,1,0:T(8,128)} async-done(((f32[2,4,512,1024]{3,2,1,0:T(8,128)}), f32[2,4,64,1024]{3,2,1,0:T(8,128)}) %reduce-scatter.21.cloned.1.call-update) | async-done | bytes 2097168 | tf_op jit(solution)/shard_map/reduce_scatter | solution.py:563
  2008.7 357.0 %reduce-scatter.19.cloned.1.call-done = f32[1,2,32,4096]{3,2,1,0:T(8,128)} async-done(((f32[1,2,1024,4096]{3,2,1,0:T(8,128)}), f32[1,2,32,4096]{3,2,1,0:T(8,128)}) %reduce-scatter.19.cloned.1.call-update) | async-done | bytes 1048592 | tf_op jit(solution)/shard_map/reduce_scatter | solution.py:559
  2367.8 357.8 %reduce-scatter.17.cloned.1.call-done = f32[1,8,32,1024]{3,1,0,2:T(8,128)} async-done(((f32[1,8,1024,1024]{3,1,0,2:T(8,128)}), f32[1,8,32,1024]{3,1,0,2:T(8,128)}) %reduce-scatter.17.cloned.1.call-update) | async-done | bytes 1048592 | tf_op jit(solution)/shard_map/reduce_scatter | solution.py:558
  2730.9 44.2 %all-reduce.6 = (f32[]{:T(128)}, f32[]{:T(128)}) all-reduce(f32[]{:T(128)} %fusion.193, f32[]{:T(128)S(6)} %add.551), channel_id=1, replica_groups=mesh['seq'=4,'fsdp'=8] {'seq','fsdp'}, use_global_device_ids=true, to_apply=%region_36.39 | all-reduce | flops 2 | bytes 16 | tf_op jit(solution)/shard_map/psum | solution.py:571
  (926 shorter events, 711.7 us)
Async XLA Ops:
  8.0 442.9 %copy-start = (bf16[1,64,1024]{2,1,0:T(8,128)(2,1)S(1)}, bf16[1,64,1024]{2,1,0:T(8,128)(2,1)}, u32[]{:S(2)}) copy-start(bf16[1,64,1024]{2,1,0:T(8,128)(2,1)} %param.46) | copy-start | bytes 393220
  8.1 83.7 %all-gather.11.cloned.1.call-start = ((), (), s32[]{:S(2)}) async-start(), calls=%async_computation.16 | async-start | bytes 9437184 | tf_op jit(solution)/shard_map/all_gather | solution.py:423
  10.8 207.8 %reduce-scatter.11.cloned.1.call-start = ((), (), s32[]{:S(2)}) async-start(), calls=%async_computation.17 | async-start | bytes 7864320 | tf_op jit(solution)/shard_map/reduce_scatter | solution.py:435
  132.9 134.2 %all-gather.13.cloned.1.call-start = ((), (), s32[]{:S(2)}) async-start(), calls=%async_computation.18 | async-start | bytes 17301504 | tf_op jit(solution)/shard_map/all_gather | solution.py:418
  135.0 357.2 %all-gather.15.cloned.1.call-start = ((), (), s32[]{:S(2)}) async-start(), calls=%async_computation.19 | async-start | bytes 17301504 | tf_op jit(solution)/shard_map/all_gather | solution.py:419
  200.2 225.9 %copy-start.144 = (f32[1024]{0:T(1024)}, f32[1024]{0:T(1024)S(1)}, u32[]{:S(2)}) copy-start(f32[1024]{0:T(1024)S(1)} %get-tuple-element.442) | copy-start | bytes 12292
  200.2 225.9 %copy-start.195 = (f32[1024]{0:T(1024)}, f32[1024]{0:T(1024)S(1)}, u32[]{:S(2)}) copy-start(f32[1024]{0:T(1024)S(1)} %get-tuple-element.441) | copy-start | bytes 12292
  200.2 291.9 %copy-start.108 = (f32[1024]{0:T(1024)}, f32[1024]{0:T(1024)S(1)}, u32[]{:S(2)}) copy-start(f32[1024]{0:T(1024)S(1)} %get-tuple-element.440) | copy-start | bytes 12292
  200.2 1103.0 %copy-start.101 = (f32[1024]{0:T(1024)}, f32[1024]{0:T(1024)S(1)}, u32[]{:S(2)}) copy-start(f32[1024]{0:T(1024)S(1)} %get-tuple-element.439) | copy-start | bytes 12292
  279.8 56.8 %all-to-all-start = ((bf16[384,3,1024]{0,1,2:T(4,128)(2,1)}), bf16[384,3,1024]{0,1,2:T(4,128)(2,1)}, u32[]{:S(2)}, u32[]{:S(2)}) async-start(bf16[384,3,1024]{0,1,2:T(4,128)(2,1)} %copy.247), calls=%async_computation.1 | async-start | bytes 6291456 | tf_op jit(solution)/shard_map/all_to_all | solution.py:67
  402.0 15.1 all-to-all-start.1
  442.3 14.6 all-to-all-start.2
  468.0 15.1 all-to-all-start.3
  473.2 59.6 %all-gather.19.cloned.1.call-start = ((), (), s32[]{:S(2)}) async-start(), calls=%async_computation.21 | async-start | bytes 2162688 | tf_op jit(solution)/shard_map/all_gather | solution.py:421
  473.9 104.9 %all-gather.17.cloned.1.call-start = ((), (), s32[]{:S(2)}) async-start(), calls=%async_computation.20 | async-start | bytes 3932160 | tf_op jit(solution)/shard_map/all_gather | solution.py:454
  491.8 811.4 %copy-start.121 = (f32[384]{0:T(512)}, f32[384]{0:T(512)S(1)}, u32[]{:S(2)}) copy-start(f32[384]{0:T(512)S(1)} %broadcast_multiply_fusion.1) | copy-start | bytes 4612
  492.1 811.1 %copy-start.128 = (f32[384]{0:T(512)}, f32[384]{0:T(512)S(1)}, u32[]{:S(2)}) copy-start(f32[384]{0:T(512)S(1)} %fusion.241) | copy-start | bytes 4612
  521.9 103.1 %all-gather.21.cloned.1.call-start = ((), (), s32[]{:S(2)}) async-start(), calls=%async_computation.22 | async-start | bytes 3932160 | tf_op jit(solution)/shard_map/all_gather | solution.py:455
  536.6 667.9 %reduce-scatter.13.cloned.1.call-start = ((), (), s32[]{:S(2)}) async-start(), calls=%async_computation.23 | async-start | bytes 7864320 | tf_op jit(solution)/shard_map/reduce_scatter | solution.py:517
  1131.7 145.7 %reduce-scatter.15.cloned.1.call-start = ((), (), s32[]{:S(2)}) async-start(), calls=%async_computation.24 | async-start | bytes 7864320 | tf_op jit(solution)/shard_map/reduce_scatter | solution.py:518
  1322.8 15.6 all-to-all-start.4
  1359.5 14.7 all-to-all-start.5
  1407.5 14.6 all-to-all-start.6
  1412.2 189.0 %all-gather.23.cloned.1.call-start = ((), (), s32[]{:S(2)}) async-start(), calls=%async_computation.27 | async-start | bytes 3932160 | tf_op jit(solution)/shard_map/all_gather | solution.py:546
  1557.1 151.3 %reduce-scatter.25.cloned.1.call-start = ((), (), s32[]{:S(2)}) async-start(), calls=%async_computation.30 | async-start | bytes 540672
  1562.1 273.0 %reduce-scatter.23.cloned.1.call-start = ((), (), s32[]{:S(2)}) async-start(), calls=%async_computation.29 | async-start | bytes 4325376 | tf_op jit(solution)/shard_map/reduce_scatter | solution.py:561
  1567.2 438.8 %reduce-scatter.21.cloned.1.call-start = ((), (), s32[]{:S(2)}) async-start(), calls=%async_computation.28 | async-start | bytes 18874368 | tf_op jit(solution)/shard_map/reduce_scatter | solution.py:563
  1619.8 745.9 %reduce-scatter.19.cloned.1.call-start = ((), (), s32[]{:S(2)}) async-start(), calls=%async_computation.26 | async-start | bytes 34603008 | tf_op jit(solution)/shard_map/reduce_scatter | solution.py:559
  1646.2 1079.4 %reduce-scatter.17.cloned.1.call-start = ((), (), s32[]{:S(2)}) async-start(), calls=%async_computation.25 | async-start | bytes 34603008 | tf_op jit(solution)/shard_map/reduce_scatter | solution.py:558
  1706.1 1069.8 %copy-start.59 = (f32[1,8,32,1024]{3,2,1,0:T(8,128)S(1)}, f32[1,8,32,1024]{3,2,1,0:T(8,128)}, u32[]{:S(2)}) copy-start(f32[1,8,32,1024]{3,2,1,0:T(8,128)} %param.48) | copy-start | bytes 3145732
  1706.1 1069.8 %copy-start.87 = (f32[1,8,32,1024]{3,2,1,0:T(8,128)S(1)}, f32[1,8,32,1024]{3,2,1,0:T(8,128)}, u32[]{:S(2)}) copy-start(f32[1,8,32,1024]{3,2,1,0:T(8,128)} %param.50) | copy-start | bytes 3145732
  1706.1 1069.8 %copy-start.88 = (f32[1,8,32,1024]{3,2,1,0:T(8,128)S(1)}, f32[1,8,32,1024]{3,2,1,0:T(8,128)}, u32[]{:S(2)}) copy-start(f32[1,8,32,1024]{3,2,1,0:T(8,128)} %param.49) | copy-start | bytes 3145732
  (268 other events, 2717.7 us)
Sparse Core Ops, SparseCore 0:
  11.0 80.6 all-gather.10
  133.0 85.6 reduce-scatter.10
  1131.8 72.6 reduce-scatter.12
  1207.3 70.0 reduce-scatter.14
  1557.2 43.9 all-gather.22
Sparse Core Ops, SparseCore 1:
  137.0 130.0 all-gather.12
  270.6 127.7 all-gather.14
  477.3 55.5 all-gather.18
  535.3 43.5 all-gather.16
  581.2 43.7 all-gather.20
  1562.2 130.2 reduce-scatter.24
  1694.6 140.4 reduce-scatter.22
  1837.3 168.6 reduce-scatter.20
  2008.1 357.5 reduce-scatter.18
  2368.0 357.5 reduce-scatter.16
where the time goes:
time: 2830 us; the launch traced here: 2810 us
  waiting for transfers between devices  1460 us (52%)
  local copies, waits for them, and re-layouts  683 us (24%)
  matrix products  290 us (10%)
  other arithmetic  162 us (6%)
  blocking collectives  151 us (5%)
  starting transfers between devices  36.9 us (1%)
    gather x8, local copies, waits for them, and re-layouts, on_device(): jnp.take_along_axis(logits, safe_targets[codebook][:, None], axis=1)[:, 0]  419 us
    reduce_scatter x1, waiting for transfers between devices, on_device(): lax.psum_scatter(attention_local, ('seq', 'fsdp'), scatter_dimension=2, t...  358 us
    reduce_scatter x1, waiting for transfers between devices, on_device(): lax.psum_scatter(feedforward_local, ('seq', 'fsdp'), scatter_dimension=2,...  357 us
    reduce_scatter x1, waiting for transfers between devices, on_device(): lax.psum_scatter(grad_tables, 'fsdp', scatter_dimension=2, tiled=True)  169 us
    reduce_scatter x1, waiting for transfers between devices, on_device(): lax.psum_scatter(grad_ahead_matrix, ('seq', 'fsdp'), scatter_dimension=0,...  125 us
    dot_general x16, matrix products, float_dot(): return jnp.dot(left, right, preferred_element_type=jnp.float32)  89.6 us
    unnamed x587, local copies, waits for them, and re-layouts  80.6 us
    all_gather x1, waiting for transfers between devices, on_device(): tables_part = lax.all_gather(tables_low, 'fsdp', axis=2, tiled=True)  79.4 us
  transfers between devices with their start and end apart: 22, of which 20 were waited for; matrix products, arithmetic and copies ran while one was open for 13% of the time, Pallas kernels for 0%

commit v1 on v0

--- a/solution.py
+++ b/solution.py
@@ -4,6 +4,8 @@
 import jax
 import jax.numpy as jnp
 from jax import lax
+from jax.experimental import pallas as pl
+from jax.experimental.pallas import tpu as pltpu
 from jax.sharding import PartitionSpec as P
 
 D = 1024
@@ -23,16 +25,6 @@
 masked_score = -1e30
 
 
-def combined_all(x, axis, combine):
-    everything = jax.tree.map(lambda part: lax.all_gather(part, axis), x)
-    first = jax.tree.map(lambda part: part[0], everything)
-
-    def turn(k, so_far):
-        return combine(so_far, jax.tree.map(lambda part: part[k], everything))
-
-    return lax.fori_loop(1, lax.axis_size(axis), turn, first)
-
-
 def float_dot(left, right):
     return jnp.dot(left, right, preferred_element_type=jnp.float32)
 
@@ -47,6 +39,224 @@
     return lax.dot_general(
         left, right, (((1,), (1,)), ((), ())), preferred_element_type=jnp.float32
     )
+
+
+def flip_bit(x, axis, bit):
+    return lax.ppermute(x, axis, [(i, i ^ bit) for i in range(lax.axis_size(axis))])
+
+
+def own_bit(axis, bit):
+    return (lax.axis_index(axis) // bit) % 2
+
+
+def bits_of(axis):
+    return [1 << k for k in range(lax.axis_size(axis).bit_length() - 1)]
+
+
+def device_dims():
+    return [("seq", bit) for bit in reversed(bits_of("seq"))] + [
+        ("fsdp", bit) for bit in reversed(bits_of("fsdp"))
+    ]
+
+
+def take_bit(x, position, value):
+    return lax.dynamic_index_in_dim(x, value, position, keepdims=False)
+
+
+def gathered(shard):
+    dims = device_dims()
+    order = [("fsdp", bit) for bit in reversed(bits_of("fsdp")[1:])]
+    order += [("seq", bit) for bit in bits_of("seq")] + [("fsdp", 1)]
+    done = []
+    state = shard
+    for pair in order:
+        came = flip_bit(state, *pair)
+        mine = own_bit(*pair) == 0
+        done = [d for d in dims if d in done or d == pair]
+        state = jnp.stack(
+            [jnp.where(mine, state, came), jnp.where(mine, came, state)], axis=1 + done.index(pair)
+        )
+    return state.reshape(shard.shape[0], -1, shard.shape[2])
+
+
+def halving(state, dims, order, lead):
+    dims = list(dims)
+    for axis, bit in order:
+        position = lead + dims.index((axis, bit))
+        mine = own_bit(axis, bit)
+        sent = take_bit(state, position, 1 - mine).astype(jnp.bfloat16)
+        came = flip_bit(sent, axis, bit)
+        state = take_bit(state, position, mine) + came.astype(jnp.float32)
+        dims.remove((axis, bit))
+    return state
+
+
+def scattered_products(pairs, row_first):
+    dims = device_dims()
+    seq_order = bits_of("seq") if row_first else bits_of("seq")[::-1]
+    order = [("fsdp", 1)] + [("seq", bit) for bit in seq_order]
+    order += [("fsdp", bit) for bit in bits_of("fsdp")[1:]]
+    first, second = dims.index(order[0]), dims.index(order[1])
+    rest = [k for k in range(len(dims)) if k not in (first, second)]
+    rows = pairs[0][0].shape[2]
+    share = rows >> len(dims)
+    half, quarter = rows // 2, rows // 4
+    splits = []
+    for left, right in pairs:
+        split = left.reshape(left.shape[:2] + (2,) * len(dims) + (share,))
+        split = split.transpose(
+            (2 + first, 0, 1, 2 + second) + tuple(2 + k for k in rest) + (2 + len(dims),)
+        )
+        splits.append(split.reshape((2,) + left.shape[:2] + (half,)))
+    mine, later = own_bit(*order[0]), own_bit(*order[1])
+
+    def products(which, start, size):
+        parts = []
+        for split, (left, right) in zip(splits, pairs):
+            part = lax.dynamic_slice_in_dim(take_bit(split, 0, which), start, size, 2)
+            parts.append(
+                lax.dot_general(
+                    part, right, (((1,), (1,)), ((0,), (0,))), preferred_element_type=jnp.float32
+                )
+            )
+        return parts
+
+    def joined(parts):
+        return parts[0] if len(parts) == 1 else jnp.concatenate(parts, axis=0)
+
+    sent = joined([part.astype(jnp.bfloat16) for part in products(1 - mine, 0, half)])
+    came = flip_bit(sent, *order[0])
+
+    def added(start):
+        there = lax.dynamic_slice_in_dim(came, start, quarter, 1).astype(jnp.float32)
+        parts, at = [], 0
+        for part in products(mine, start, quarter):
+            parts.append(part + there[at : at + part.shape[0]])
+            at += part.shape[0]
+        return parts
+
+    onward = joined([part.astype(jnp.bfloat16) for part in added((1 - later) * quarter)])
+    arrived = flip_bit(onward, *order[1])
+    state = joined(added(later * quarter)) + arrived.astype(jnp.float32)
+    state = state.reshape((state.shape[0],) + (2,) * len(rest) + (share, state.shape[2]))
+    return halving(state, [dims[k] for k in rest], order[2:], 1)
+
+
+def scattered_tables(full):
+    dims = [("fsdp", bit) for bit in reversed(bits_of("fsdp"))]
+    count, rows, width = full.shape
+    state = full.reshape((count,) + (2,) * len(dims) + (rows >> len(dims), width))
+    return halving(state, dims, dims[::-1], 1)
+
+
+def summed_everywhere(x):
+    for axis, bit in device_dims():
+        x = x + flip_bit(x, axis, bit)
+    return x
+
+
+def by_partner(x):
+    bits = bits_of("seq")
+    shape = x.shape
+    x = x.reshape(shape[:-1] + (2,) * len(bits) + (-1,))
+    for k, bit in enumerate(reversed(bits)):
+        axis = len(shape) - 1 + k
+        x = jnp.where(own_bit("seq", bit) == 1, jnp.flip(x, axis), x)
+    return x.reshape(shape)
+
+
+def column_orders(width):
+    bits = bits_of("seq")
+    return [(0, width // 2, bits), (width // 2, width, bits[::-1])]
+
+
+def partner_rows(rows):
+    bits = bits_of("seq")[::-1]
+    outs = []
+    for start, stop, order in column_orders(rows.shape[1]):
+        state, done = rows[:, start:stop], []
+        for bit in order:
+            done = [b for b in bits if b in done or b == bit]
+            state = jnp.stack([state, flip_bit(state, "seq", bit)], axis=done.index(bit))
+        outs.append(state.reshape(-1, stop - start))
+    return jnp.concatenate(outs, axis=1)
+
+
+def partner_sum(parts):
+    bits = bits_of("seq")[::-1]
+    outs = []
+    for start, stop, order in column_orders(parts.shape[1]):
+        left = list(bits)
+        state = parts[:, start:stop].reshape((2,) * len(bits) + (-1, stop - start))
+        for bit in order:
+            axis = left.index(bit)
+            sent = lax.index_in_dim(state, 1, axis, keepdims=False)
+            state = lax.index_in_dim(state, 0, axis, keepdims=False) + flip_bit(sent, "seq", bit)
+            left.remove(bit)
+        outs.append(state)
+    return jnp.concatenate(outs, axis=1)
+
+
+def spread_kernel(tile_ref, all_ref, send_sem, recv_sem):
+    seq_count, fsdp_count = lax.axis_size("seq"), lax.axis_size("fsdp")
+    count = seq_count * fsdp_count
+    me = lax.axis_index("seq") * fsdp_count + lax.axis_index("fsdp")
+
+    def place(k):
+        return {"seq": k // fsdp_count, "fsdp": lax.rem(k, fsdp_count)}
+
+    barrier = pltpu.get_barrier_semaphore()
+
+    def greet(k, carry):
+        pl.semaphore_signal(
+            barrier,
+            inc=1,
+            device_id=place(lax.rem(me + k, count)),
+            device_id_type=pl.DeviceIdType.MESH,
+        )
+        return carry
+
+    lax.fori_loop(1, count, greet, 0)
+    pl.semaphore_wait(barrier, count - 1)
+
+    def copy(k):
+        return pltpu.make_async_remote_copy(
+            src_ref=tile_ref,
+            dst_ref=all_ref.at[me],
+            send_sem=send_sem.at[k],
+            recv_sem=recv_sem.at[k],
+            device_id=place(lax.rem(me + k, count)),
+            device_id_type=pl.DeviceIdType.MESH,
+        )
+
+    def send(k, carry):
+        copy(k).start()
+        return carry
+
+    def wait(k, carry):
+        copy(k).wait()
+        return carry
+
+    lax.fori_loop(1, count, send, 0)
+    all_ref[me] = tile_ref[...]
+    lax.fori_loop(1, count, wait, 0)
+
+
+def spread(tile, collective_id):
+    count = lax.axis_size("seq") * lax.axis_size("fsdp")
+    return pl.pallas_call(
+        spread_kernel,
+        out_shape=jax.ShapeDtypeStruct((count,) + tile.shape, tile.dtype),
+        in_specs=[pl.BlockSpec(memory_space=pltpu.VMEM)],
+        out_specs=pl.BlockSpec(memory_space=pltpu.VMEM),
+        scratch_shapes=[pltpu.SemaphoreType.DMA((count,)), pltpu.SemaphoreType.DMA((count,))],
+        compiler_params=pltpu.CompilerParams(collective_id=collective_id, has_side_effects=True),
+        name=f"spread_{collective_id}",
+    )(tile)
+
+
+def as_tile(values):
+    return jnp.pad(values, (0, 1024 - values.shape[0])).reshape(8, 128)
 
 
 def layer_norm(residual, gain, bias):
@@ -63,12 +273,20 @@
     return jnp.concatenate([jnp.cos(places), jnp.sin(places)], axis=1)
 
 
-def to_heads(blocks):
-    return lax.all_to_all(blocks, "seq", split_axis=2, concat_axis=0, tiled=True)
-
-
-def to_rows(blocks):
-    return lax.all_to_all(blocks, "seq", split_axis=0, concat_axis=2, tiled=True)
+def to_heads(rows):
+    count = lax.axis_size("seq")
+    tokens, width = rows.shape
+    blocks = rows.reshape(tokens, count, width // count).transpose(1, 0, 2)
+    blocks = lax.all_to_all(blocks, "seq", split_axis=0, concat_axis=0, tiled=True)
+    return blocks.reshape(count * tokens, width // count)
+
+
+def to_rows(heads):
+    count = lax.axis_size("seq")
+    tokens, width = heads.shape[0] // count, heads.shape[1]
+    blocks = heads.reshape(count, tokens, width)
+    blocks = lax.all_to_all(blocks, "seq", split_axis=0, concat_axis=0, tiled=True)
+    return blocks.transpose(1, 0, 2).reshape(tokens, count * width)
 
 
 def block_size():
@@ -197,24 +415,23 @@
 def layer_forward(residual, gathered, text_clip, seq_index, seq_count):
     matrices, feedforward_w, norm_params = gathered
     norm_float = norm_params.astype(jnp.float32)
-    head_width = matrices.shape[2] // seq_count
+    head_width = matrices[0].shape[1] // seq_count
     heads_here = head_width // HD
     text_rows = text_clip.shape[0]
     normed_self = layer_norm(residual, norm_float[0, 0], norm_float[0, 1]).astype(jnp.bfloat16)
-    projected = jnp.einsum(
-        "rd,jde->rje", normed_self, matrices[0:3], preferred_element_type=jnp.float32
-    )
-    heads_qkv = to_heads(projected.astype(jnp.bfloat16))
-    total_rows = heads_qkv.shape[0]
-    queries = heads_qkv[:, 0].reshape(total_rows, heads_here, HD)
-    key_rows = heads_qkv[:, 1].reshape(total_rows, heads_here, HD)
-    value_rows = heads_qkv[:, 2].reshape(total_rows, heads_here, HD)
+    queries, key_rows, value_rows = (
+        to_heads(float_dot(normed_self, matrices[k]).astype(jnp.bfloat16)).reshape(
+            -1, heads_here, HD
+        )
+        for k in range(3)
+    )
+    total_rows = queries.shape[0]
     attended, self_totals = causal_forward(queries, key_rows, value_rows)
-    self_rows = to_rows(attended.astype(jnp.bfloat16).reshape(total_rows, 1, head_width))[:, 0]
+    self_rows = to_rows(attended.astype(jnp.bfloat16).reshape(total_rows, head_width))
     after_self = residual + float_dot(self_rows, matrices[3])
     normed_cross = layer_norm(after_self, norm_float[1, 0], norm_float[1, 1]).astype(jnp.bfloat16)
     cross_query = float_dot(normed_cross, matrices[4]).astype(jnp.bfloat16)
-    cross_heads = to_heads(cross_query[:, None, :])[:, 0].reshape(total_rows, heads_here, HD)
+    cross_heads = to_heads(cross_query).reshape(total_rows, heads_here, HD)
     column_start = seq_index * head_width
     key_columns = lax.dynamic_slice_in_dim(matrices[5], column_start, head_width, 1)
     value_columns = lax.dynamic_slice_in_dim(matrices[6], column_start, head_width, 1)
@@ -225,7 +442,7 @@
         float_dot(text_clip, value_columns).astype(jnp.bfloat16).reshape(text_rows, heads_here, HD)
     )
     cross_out, cross_totals = cross_forward(cross_heads, cross_keys, cross_values)
-    cross_rows = to_rows(cross_out.astype(jnp.bfloat16).reshape(total_rows, 1, head_width))[:, 0]
+    cross_rows = to_rows(cross_out.astype(jnp.bfloat16).reshape(total_rows, head_width))
     after_cross = after_self + float_dot(cross_rows, matrices[7])
     normed_feed = layer_norm(after_cross, norm_float[2, 0], norm_float[2, 1]).astype(jnp.bfloat16)
     hidden_pre = float_dot(normed_feed, feedforward_w[0])
@@ -253,7 +470,9 @@
     return (output, saved)
 
 
-def layer_backward(residual, gathered, text_clip, saved, grad_residual, seq_index, seq_count):
+def layer_backward(
+    residual, gathered, text_clip, saved, grad_residual, seq_index, seq_count, ahead_left, ahead_right
+):
     matrices, feedforward_w, norm_params = gathered
     norm_float = norm_params.astype(jnp.float32)
     (
@@ -275,75 +494,67 @@
         hidden_pre,
         hidden_low,
     ) = saved
-    head_width = matrices.shape[2] // seq_count
+    head_width = matrices[0].shape[1] // seq_count
     heads_here = head_width // HD
     total_rows = queries.shape[0]
     text_rows = text_clip.shape[0]
     column_start = seq_index * head_width
     branch_low = grad_residual.astype(jnp.bfloat16)
-    grad_down = dot_first(branch_low, hidden_low)
+    down_left = branch_low
     grad_hidden = float_dot(branch_low, feedforward_w[1])
     unused_gelu, gelu_pull = jax.vjp(partial(jax.nn.gelu, approximate=False), hidden_pre)
     grad_pre = gelu_pull(grad_hidden)[0].astype(jnp.bfloat16)
-    grad_up = dot_first(normed_feed, grad_pre)
+    feed_grads = scattered_products(
+        [(normed_feed[None], grad_pre[None]), (down_left[None], hidden_low[None])], True
+    )
     grad_normed = dot_last(grad_pre, feedforward_w[0])
     unused_norm, norm_pull = jax.vjp(layer_norm, after_cross, norm_float[2, 0], norm_float[2, 1])
     grad_inner, feed_gain, feed_bias = norm_pull(grad_normed)
     grad_residual = grad_residual + grad_inner
     branch_low = grad_residual.astype(jnp.bfloat16)
-    grad_cross_out = dot_first(cross_rows, branch_low)
+    cross_branch = branch_low
     grad_rows = dot_last(branch_low, matrices[7]).astype(jnp.bfloat16)
-    grad_heads = to_heads(grad_rows[:, None, :])[:, 0].reshape(total_rows, heads_here, HD)
+    grad_heads = to_heads(grad_rows).reshape(total_rows, heads_here, HD)
     grad_cq, grad_ck, grad_cv = cross_backward(
         cross_heads, cross_keys, cross_values, cross_totals, grad_heads
     )
-    grad_cq_rows = to_rows(grad_cq.astype(jnp.bfloat16).reshape(total_rows, 1, head_width))[:, 0]
-    grad_cross_query = dot_first(normed_cross, grad_cq_rows)
+    grad_cq_rows = to_rows(grad_cq.astype(jnp.bfloat16).reshape(total_rows, head_width))
     grad_normed = dot_last(grad_cq_rows, matrices[4])
     key_low = grad_ck.reshape(text_rows, head_width).astype(jnp.bfloat16)
     value_low = grad_cv.reshape(text_rows, head_width).astype(jnp.bfloat16)
-    zero_matrix = jnp.zeros((matrices.shape[1], matrices.shape[2]), jnp.float32)
-    grad_cross_keys = lax.dynamic_update_slice_in_dim(
-        zero_matrix, dot_first(text_clip, key_low), column_start, 1
-    )
-    grad_cross_values = lax.dynamic_update_slice_in_dim(
-        zero_matrix, dot_first(text_clip, value_low), column_start, 1
-    )
+    wide = jnp.zeros((text_rows, head_width * seq_count), jnp.bfloat16)
+    wide_key = lax.dynamic_update_slice(wide, key_low, (0, column_start))
+    wide_value = lax.dynamic_update_slice(wide, value_low, (0, column_start))
     unused_norm, norm_pull = jax.vjp(layer_norm, after_self, norm_float[1, 0], norm_float[1, 1])
     grad_inner, cross_gain, cross_bias = norm_pull(grad_normed)
     grad_residual = grad_residual + grad_inner
     branch_low = grad_residual.astype(jnp.bfloat16)
-    grad_self_out = dot_first(self_rows, branch_low)
+    early_grads = scattered_products(
+        [
+            (self_rows[None], branch_low[None]),
+            (normed_cross[None], grad_cq_rows[None]),
+            (jnp.stack([text_clip, text_clip]), jnp.stack([wide_key, wide_value])),
+            (cross_rows[None], cross_branch[None]),
+            (ahead_left[None], ahead_right[None]),
+        ],
+        False,
+    )
     grad_rows = dot_last(branch_low, matrices[3]).astype(jnp.bfloat16)
-    grad_heads = to_heads(grad_rows[:, None, :])[:, 0].reshape(total_rows, heads_here, HD)
+    grad_heads = to_heads(grad_rows).reshape(total_rows, heads_here, HD)
     grad_q, grad_k, grad_v = causal_backward(queries, key_rows, value_rows, self_totals, grad_heads)
-    stacked = (
-        jnp.stack([grad_q, grad_k, grad_v], axis=1)
-        .reshape(total_rows, 3, head_width)
-        .astype(jnp.bfloat16)
-    )
-    grad_qkv_rows = to_rows(stacked)
-    grad_qkv = jnp.einsum(
-        "rd,rje->jde", normed_self, grad_qkv_rows, preferred_element_type=jnp.float32
-    )
-    grad_normed = jnp.einsum(
-        "rje,jde->rd", grad_qkv_rows, matrices[0:3], preferred_element_type=jnp.float32
+    grad_parts = [
+        to_rows(part.astype(jnp.bfloat16).reshape(total_rows, head_width))
+        for part in (grad_q, grad_k, grad_v)
+    ]
+    late_grads = scattered_products([(normed_self[None], part[None]) for part in grad_parts], True)
+    grad_normed = (
+        dot_last(grad_parts[0], matrices[0])
+        + dot_last(grad_parts[1], matrices[1])
+        + dot_last(grad_parts[2], matrices[2])
     )
     unused_norm, norm_pull = jax.vjp(layer_norm, residual, norm_float[0, 0], norm_float[0, 1])
     grad_inner, self_gain, self_bias = norm_pull(grad_normed)
     grad_residual = grad_residual + grad_inner
-    grad_matrices = jnp.concatenate(
-        [
-            grad_qkv,
-            grad_self_out[None],
-            grad_cross_query[None],
-            grad_cross_keys[None],
-            grad_cross_values[None],
-            grad_cross_out[None],
-        ],
-        axis=0,
-    )
-    grad_feed = jnp.stack([grad_up, grad_down], axis=0)
     grad_norms = jnp.stack(
         [
             jnp.stack([self_gain, self_bias]),
@@ -352,17 +563,7 @@
         ],
         axis=0,
     )
-    return (grad_residual, grad_matrices, grad_feed, grad_norms)
-
-
-def combine_stats(first, second):
-    first_max, first_sum, first_pick = first
-    second_max, second_sum, second_pick = second
-    joint_max = jnp.maximum(first_max, second_max)
-    joint_sum = first_sum * jnp.exp(first_max - joint_max) + second_sum * jnp.exp(
-        second_max - joint_max
-    )
-    return (joint_max, joint_sum, first_pick + second_pick)
+    return (grad_residual, late_grads, early_grads, feed_grads, grad_norms)
 
 
 def adamw_update(master, mean, square, gradient, factor, first_fix, second_fix, decay):
@@ -414,46 +615,42 @@
     tables_low = tables_master.astype(jnp.bfloat16)
     ahead_low = ahead_master.astype(jnp.bfloat16)
     norms_low = norms_master.astype(jnp.bfloat16)
-    attention_all, feedforward_all, norms_all, ahead_full = (
-        lax.all_gather(attention_low, ("seq", "fsdp"), axis=2, tiled=True),
-        lax.all_gather(feedforward_low, ("seq", "fsdp"), axis=2, tiled=True),
-        lax.all_gather(norms_low, ("seq", "fsdp"), axis=2, tiled=True),
-        lax.all_gather(ahead_low, ("seq", "fsdp"), axis=0, tiled=True),
-    )
-    tables_part = lax.all_gather(tables_low, "fsdp", axis=2, tiled=True)
-    final_norm = norms_all[3 * LAYERS]
-    vocab_part = tables_part.shape[2]
+    share = norms_low.shape[2]
+    norms_all = (
+        spread(as_tile(norms_low.astype(jnp.float32).reshape(-1)), 0)
+        .reshape(-1, 1024)[:, : norms_low.size]
+        .reshape((-1,) + norms_low.shape)
+        .transpose(1, 2, 0, 3)
+        .reshape(norms_low.shape[0], 2, D)
+    )
+    qkv_all = gathered(attention_low[0, :3])
+    embed_part = lax.all_gather(tables_low[0], "fsdp", axis=1, tiled=True)
+    vocab_part = embed_part.shape[1]
     vocab_start = seq_index * vocab_part
     vocab_range = jnp.arange(vocab_part, dtype=jnp.int32)
-    local_ids = codes_clip - vocab_start
-    inside = (local_ids >= 0) & (local_ids < vocab_part)
-    safe_ids = jnp.where(inside, local_ids, 0)
-    embed_sum = jnp.zeros((total_rows, D), jnp.float32)
-    for codebook in range(CODEBOOKS):
-        looked = jnp.take(tables_part[0, codebook], safe_ids[codebook], axis=0).astype(jnp.float32)
-        embed_sum = embed_sum + jnp.where(inside[codebook][:, None], looked, 0.0)
-    embedded = lax.psum_scatter(embed_sum, "seq", scatter_dimension=0, tiled=True)
-    residual = embedded + sinusoids(row_start.astype(jnp.float32), rows_here, D)
-
-    def layer_of(layer_index):
-        return (
-            attention_all[layer_index],
-            feedforward_all[layer_index],
-            norms_all[3 * layer_index : 3 * layer_index + 3],
-        )
-
-    layer_index = 0
-    layer_inputs = [residual]
-    residual, unused_saved = layer_forward(
-        residual, layer_of(layer_index), text_clip, seq_index, seq_count
-    )
-    final_float = final_norm.astype(jnp.float32)
+    local_ids = by_partner(codes_clip) - vocab_start
+    onehot_ids = (
+        (local_ids.T[:, :, None] == vocab_range[None, None, :])
+        .astype(jnp.bfloat16)
+        .reshape(total_rows, CODEBOOKS * vocab_part)
+    )
+    embed_sum = float_dot(onehot_ids, embed_part.reshape(CODEBOOKS * vocab_part, D))
+    residual = partner_sum(embed_sum) + sinusoids(row_start.astype(jnp.float32), rows_here, D)
+    both = ("seq", "fsdp")
+    matrices = [qkv_all[k] for k in range(3)] + [
+        lax.all_gather(attention_low[0, k], both, axis=0, tiled=True) for k in range(3, 8)
+    ]
+    feed_all = [lax.all_gather(feedforward_low[0, k], both, axis=0, tiled=True) for k in range(2)]
+    ahead_full = lax.all_gather(ahead_low, both, axis=0, tiled=True)
+    heads_part = lax.all_gather(tables_low[1], "fsdp", axis=1, tiled=True)
+    heads_rows = heads_part.reshape(CODEBOOKS * vocab_part, D)
+    gathered_layer = (matrices, feed_all, norms_all[:3])
+    final_float = norms_all[3 * LAYERS]
+    layer_input = residual
+    residual, saved = layer_forward(residual, gathered_layer, text_clip, seq_index, seq_count)
     final_low = layer_norm(residual, final_float[0], final_float[1]).astype(jnp.bfloat16)
-    ahead_rows = float_dot(final_low, ahead_full).astype(jnp.bfloat16)
-    final_all, ahead_all = (
-        lax.all_gather(final_low, "seq", axis=0, tiled=True),
-        lax.all_gather(ahead_rows, "seq", axis=0, tiled=True),
-    )
+    final_all = partner_rows(final_low)
+    ahead_all = float_dot(final_all, ahead_full).astype(jnp.bfloat16)
     frames = jnp.arange(total_rows, dtype=jnp.int32)
     target_sets = []
     for target_shift in (1, 2):
@@ -461,106 +658,75 @@
         targets = jnp.concatenate([codes_clip[:, target_shift:], padding], axis=1)
         live_mask = jnp.concatenate([masks_clip[:, target_shift:], padding], axis=1)
         live_mask = live_mask * (frames + target_shift < length_clip).astype(jnp.int32)
-        local_targets = targets - vocab_start
-        target_inside = (local_targets >= 0) & (local_targets < vocab_part)
-        safe_targets = jnp.where(target_inside, local_targets, 0)
-        target_sets.append((safe_targets, target_inside, live_mask.astype(jnp.float32)))
+        target_sets.append(
+            (by_partner(targets) - vocab_start, by_partner(live_mask).astype(jnp.float32))
+        )
     sources = (final_all, ahead_all)
     logit_blocks = []
-    maxima = []
-    sums = []
-    picks = []
+    stats = []
     for objective_index in range(2):
-        safe_targets, target_inside, live_mask = target_sets[objective_index]
+        local_targets, live_mask = target_sets[objective_index]
         for codebook in range(CODEBOOKS):
-            logits = dot_last(sources[objective_index], tables_part[1, codebook])
+            logits = dot_last(sources[objective_index], heads_part[codebook])
             row_max = jnp.max(logits, axis=1)
             row_sum = jnp.sum(jnp.exp(logits - row_max[:, None]), axis=1)
-            picked = jnp.take_along_axis(logits, safe_targets[codebook][:, None], axis=1)[:, 0]
+            hit = vocab_range[None, :] == local_targets[codebook][:, None]
+            picked = jnp.sum(jnp.where(hit, logits, 0.0), axis=1)
             logit_blocks.append(logits)
-            maxima.append(row_max)
-            sums.append(row_sum)
-            picks.append(jnp.where(target_inside[codebook], picked, 0.0))
-    merged_max, merged_sum, merged_pick = combined_all(
-        (jnp.stack(maxima), jnp.stack(sums), jnp.stack(picks)), "seq", combine_stats
-    )
+            stats.append(jnp.stack([row_max, row_sum, picked]))
+    own_stats = by_partner(jnp.stack(stats, axis=1))
+    all_stats = lax.all_gather(own_stats.reshape(-1, total_rows), "seq")
+    all_stats = by_partner(all_stats.reshape((seq_count,) + own_stats.shape))
+    merged_max = jnp.max(all_stats[:, 0], axis=0)
+    merged_sum = jnp.sum(all_stats[:, 1] * jnp.exp(all_stats[:, 0] - merged_max), axis=0)
+    merged_pick = jnp.sum(all_stats[:, 2], axis=0)
     log_totals = merged_max + jnp.log(merged_sum)
     factors = jnp.array([1.0] * CODEBOOKS + [ahead_weight] * CODEBOOKS, jnp.float32)[:, None]
-    weighted = factors * jnp.concatenate([target_sets[0][2], target_sets[1][2]], axis=0)
-    own_terms = lax.dynamic_slice_in_dim(
-        weighted * (log_totals - merged_pick), row_start, rows_here, 1
-    )
-    own_loss = jnp.sum(own_terms)
-    grad_final_part = jnp.zeros((total_rows, D), jnp.float32)
-    grad_ahead_part = jnp.zeros((total_rows, D), jnp.float32)
-    head_grads = [jnp.zeros((vocab_part, D), jnp.float32) for codebook in range(CODEBOOKS)]
+    weighted = factors * jnp.concatenate([target_sets[0][1], target_sets[1][1]], axis=0)
+    own_loss = jnp.sum((weighted * (log_totals - merged_pick))[:, :rows_here])
+    grad_parts = []
+    head_grads = None
     for objective_index in range(2):
-        safe_targets, target_inside, live_mask = target_sets[objective_index]
+        local_targets, live_mask = target_sets[objective_index]
+        lows = []
         for codebook in range(CODEBOOKS):
             position = objective_index * CODEBOOKS + codebook
-            attention_probs = jnp.exp(logit_blocks[position] - log_totals[position][:, None])
-            onehot = (
-                (vocab_range[None, :] == safe_targets[codebook][:, None])
-                & target_inside[codebook][:, None]
-            ).astype(jnp.float32)
+            probs = jnp.exp(logit_blocks[position] - log_totals[position][:, None])
+            onehot = (vocab_range[None, :] == local_targets[codebook][:, None]).astype(jnp.float32)
             coefficient = (weighted[position] * scale_norm)[:, None]
-            grad_low = (coefficient * (attention_probs - onehot)).astype(jnp.bfloat16)
-            part_rows = float_dot(grad_low, tables_part[1, codebook])
-            if objective_index == 0:
-                grad_final_part = grad_final_part + part_rows
-            else:
-                grad_ahead_part = grad_ahead_part + part_rows
-            head_grads[codebook] = head_grads[codebook] + dot_first(
-                grad_low, sources[objective_index]
-            )
-    grad_final_rows, grad_ahead_rows = (
-        lax.psum_scatter(grad_final_part, "seq", scatter_dimension=0, tiled=True),
-        lax.psum_scatter(grad_ahead_part, "seq", scatter_dimension=0, tiled=True),
-    )
-    ahead_grad_low = grad_ahead_rows.astype(jnp.bfloat16)
-    grad_ahead_matrix = dot_first(final_low, ahead_grad_low)
-    grad_final = grad_final_rows + dot_last(ahead_grad_low, ahead_full)
+            lows.append((coefficient * (probs - onehot)).astype(jnp.bfloat16))
+        grad_low = jnp.concatenate(lows, axis=1)
+        grad_parts.append(float_dot(grad_low, heads_rows))
+        product = dot_first(grad_low, sources[objective_index])
+        head_grads = product if head_grads is None else head_grads + product
+    heads_shard = scattered_tables(head_grads.reshape(CODEBOOKS, vocab_part, D))
+    ahead_grad_low = grad_parts[1].astype(jnp.bfloat16)
+    grad_final = partner_sum(grad_parts[0] + dot_last(ahead_grad_low, ahead_full))
     unused_norm, final_pull = jax.vjp(layer_norm, residual, final_float[0], final_float[1])
     grad_residual, final_gain, final_bias = final_pull(grad_final)
-    matrix_grads = [None] * LAYERS
-    feed_grads = [None] * LAYERS
-    norm_grads = [None] * LAYERS
-    for layer_index in reversed(range(LAYERS)):
-        gathered = layer_of(layer_index)
-        unused_output, saved = layer_forward(
-            layer_inputs[layer_index], gathered, text_clip, seq_index, seq_count
-        )
-        grad_residual, grad_matrices, grad_feed, grad_norms = layer_backward(
-            layer_inputs[layer_index],
-            gathered,
-            text_clip,
-            saved,
-            grad_residual,
-            seq_index,
-            seq_count,
-        )
-        matrix_grads[layer_index] = grad_matrices
-        feed_grads[layer_index] = grad_feed
-        norm_grads[layer_index] = grad_norms
-    embed_grad_low = grad_residual.astype(jnp.bfloat16)
-    embed_grad_all = lax.all_gather(embed_grad_low, "seq", axis=0, tiled=True)
-    embed_grads = []
-    for codebook in range(CODEBOOKS):
-        onehot_ids = (
-            (safe_ids[codebook][:, None] == vocab_range[None, :]) & inside[codebook][:, None]
-        ).astype(jnp.bfloat16)
-        embed_grads.append(dot_first(onehot_ids, embed_grad_all))
-    grad_tables = jnp.stack([jnp.stack(embed_grads), jnp.stack(head_grads)])
-    attention_local = jnp.stack(matrix_grads)
-    feedforward_local = jnp.stack(feed_grads)
-    norms_local = jnp.concatenate(norm_grads + [jnp.stack([final_gain, final_bias])[None]], axis=0)
-    attention_grad, feedforward_grad, norms_grad, ahead_grad_shard = (
-        lax.psum_scatter(attention_local, ("seq", "fsdp"), scatter_dimension=2, tiled=True),
-        lax.psum_scatter(feedforward_local, ("seq", "fsdp"), scatter_dimension=2, tiled=True),
-        lax.psum_scatter(norms_local, ("seq", "fsdp"), scatter_dimension=2, tiled=True),
-        lax.psum_scatter(grad_ahead_matrix, ("seq", "fsdp"), scatter_dimension=0, tiled=True),
-    )
-    tables_grad_shard = lax.psum_scatter(grad_tables, "fsdp", scatter_dimension=2, tiled=True)
+    grad_residual, late_grads, early_grads, feedforward_grad, norm_grads = layer_backward(
+        layer_input,
+        gathered_layer,
+        text_clip,
+        saved,
+        grad_residual,
+        seq_index,
+        seq_count,
+        final_all,
+        ahead_grad_low,
+    )
+    embed_grad_all = partner_rows(grad_residual.astype(jnp.bfloat16))
+    embed_grads = dot_first(onehot_ids, embed_grad_all)
+    embed_shard = scattered_tables(embed_grads.reshape(CODEBOOKS, vocab_part, D))
+    tables_grad_shard = jnp.stack([embed_shard, heads_shard])
+    attention_grad = jnp.concatenate([late_grads, early_grads[:5]], axis=0)[None]
+    feedforward_grad = feedforward_grad[None]
+    ahead_grad_shard = early_grads[5]
+    norms_local = jnp.concatenate([norm_grads, jnp.stack([final_gain, final_bias])[None]], axis=0)
+    norms_total = summed_everywhere(norms_local.reshape(-1, D))
+    place = seq_index * clips_total + lax.axis_index("fsdp")
+    norms_grad = lax.dynamic_slice_in_dim(norms_total, place * share, share, 1)
+    norms_grad = norms_grad.reshape(norms_master.shape)
     squares = (
         jnp.sum(attention_grad * attention_grad)
         + jnp.sum(feedforward_grad * feedforward_grad)
@@ -568,7 +734,8 @@
         + jnp.sum(ahead_grad_shard * ahead_grad_shard)
         + jnp.sum(norms_grad * norms_grad)
     )
-    total_squares, total_loss = lax.psum((squares, own_loss), ("seq", "fsdp"))
+    totals = jnp.sum(spread(as_tile(jnp.stack([squares, own_loss])), 1)[:, 0, :2], axis=0)
+    total_squares, total_loss = totals[0], totals[1]
     gradient_norm = jnp.sqrt(total_squares)
     loss_value = total_loss * scale_norm
     factor = jnp.minimum(1.0, clip_limit / (gradient_norm + 1e-06))

time: 2830 us -> 1380 us (0.49)
  waiting for transfers between devices: 1460 us -> 526 us
  local copies, waits for them, and re-layouts: 683 us -> 136 us
  blocking collectives: 151 us -> 10.1 us
  starting transfers between devices: 36.9 us -> 101 us
  Pallas kernels: 0 us -> 55.1 us
  matrix products: 290 us -> 325 us
    reduce_scatter x7 -> x0, waiting for transfers between devices: 1150 us -> none  [the longest x1 358 us: on_device(): lax.psum_scatter(attention_local, ('seq', 'fsdp'), scatter_dimension=2, t...]
    gather x12 -> x0, local copies, waits for them, and re-layouts: 445 us -> none  [the longest x8 419 us: on_device(): jnp.take_along_axis(logits, safe_targets[codebook][:, None], axis=1)[:, 0]]
    ppermute x0 -> x47, waiting for transfers between devices: none -> 325 us  [flip_bit(): lax.ppermute(x, axis, [(i, i ^ bit) for i in range(lax.axis_size(axis))])]
    all_to_all x7 -> x12, waiting for transfers between devices: 95.7 us -> 30 us  [the longest x6 16.5 us: to_rows(): lax.all_to_all(blocks, 'seq', split_axis=0, concat_axis=0, tiled=True)]
    all_gather x4 -> x1, blocking collectives: 67.6 us -> 10.1 us  [on_device(): all_stats = lax.all_gather(own_stats.reshape(-1, total_rows), 'seq')]
    pallas_call x0 -> x2, Pallas kernels: none -> 55.1 us  [spread(): pl.pallas_call(spread_kernel, out_shape=jax.ShapeDtypeStruct((count,) + t...]
    ppermute x0 -> x47, starting transfers between devices: none -> 47.9 us  [flip_bit(): lax.ppermute(x, axis, [(i, i ^ bit) for i in range(lax.axis_size(axis))])]
    unnamed x587 -> x466, local copies, waits for them, and re-layouts: 80.6 us -> 34.4 us
  transfers between devices with their start and end apart: 22 -> 69, of which waited for: 20 -> 36; matrix products, arithmetic and copies ran while one was open for 13% -> 37% of each run, Pallas kernels for 0% -> 3%
where the time goes in v1:
time: 1380 us; the launch traced here: 1370 us
  waiting for transfers between devices  526 us (38%)
  matrix products  325 us (24%)
  other arithmetic  188 us (14%)
  local copies, waits for them, and re-layouts  136 us (10%)
  starting transfers between devices  101 us (7%)
  Pallas kernels  55.1 us (4%)
  between operations  27 us (2%)
    ppermute x47, waiting for transfers between devices, flip_bit(): lax.ppermute(x, axis, [(i, i ^ bit) for i in range(lax.axis_size(axis))])  325 us
    all_gather x2, waiting for transfers between devices, on_device(): lax.all_gather(feedforward_low[0, k], both, axis=0, tiled=True)  133 us
    dot_general x14, matrix products, float_dot(): return jnp.dot(left, right, preferred_element_type=jnp.float32)  80.2 us
    dot_general x17, matrix products, dot_last(): lax.dot_general(left, right, (((1,), (1,)), ((), ())), preferred_element_...  79.9 us
    dot_general x30, matrix products, products(): lax.dot_general(part, right, (((1,), (1,)), ((0,), (0,))), preferred_elem...  62.3 us
    pallas_call x2, Pallas kernels, spread(): pl.pallas_call(spread_kernel, out_shape=jax.ShapeDtypeStruct((count,) + t...  55.1 us
    ppermute x47, starting transfers between devices, flip_bit(): lax.ppermute(x, axis, [(i, i ^ bit) for i in range(lax.axis_size(axis))])  47.9 us
    unnamed x466, local copies, waits for them, and re-layouts  34.4 us
  transfers between devices with their start and end apart: 69, of which 36 were waited for; matrix products, arithmetic and copies ran while one was open for 37% of the time, Pallas kernels for 3%

profile of v1, /device:TPU:12, one launch (start us, length us, event | category | flops | bytes accessed | tf_op | source)
XLA Modules:
  0.0 1368.3 jit_solution(5457578446785029951)
XLA Ops:
  18.7 21.1 %collective-permute-done.4 = bf16[3,32,1024]{2,1,0:T(8,128)(2,1)S(1)} collective-permute-done((bf16[3,32,1024]{2,1,0:T(8,128)(2,1)S(1)}, bf16[3,32,1024]{2,1,0:T(8,128)(2,1)S(1)}, u32[]{:S(2)}, u32[]{:S(2)}) %collective-permute-start.4) | collective-permute-done | bytes 196640 | tf_op jit(solution)/shard_map/ppermute | solution.py:45
  41.4 23.7 %collective-permute-done.5 = bf16[3,2,32,1024]{3,2,1,0:T(8,128)(2,1)S(1)} collective-permute-done((bf16[3,2,32,1024]{3,2,1,0:T(8,128)(2,1)S(1)}, bf16[3,2,32,1024]{3,2,1,0:T(8,128)(2,1)S(1)}, u32[]{:S(2)}, u32[]{:S(2)}) %collective-permute-start.5) | collective-permute-done | bytes 393248 | tf_op jit(solution)/shard_map/ppermute | solution.py:45
  66.8 18.1 %collective-permute-done.6 = bf16[3,2,2,32,1024]{4,3,2,1,0:T(8,128)(2,1)S(1)} collective-permute-done((bf16[3,2,2,32,1024]{4,3,2,1,0:T(8,128)(2,1)S(1)}, bf16[3,2,2,32,1024]{4,3,2,1,0:T(8,128)(2,1)S(1)}, u32[]{:S(2)}, u32[]{:S(2)}) %collective-permute-start.6) | collective-permute-done | bytes 786464 | tf_op jit(solution)/shard_map/ppermute | solution.py:45
  88.7 37.0 %collective-permute-done.7 = bf16[3,2,2,2,32,1024]{5,4,3,2,1,0:T(8,128)(2,1)} collective-permute-done((bf16[3,2,2,2,32,1024]{5,4,3,2,1,0:T(8,128)(2,1)S(1)}, bf16[3,2,2,2,32,1024]{5,4,3,2,1,0:T(8,128)(2,1)}, u32[]{:S(2)}, u32[]{:S(2)}) %collective-permute-start.7) | collective-permute-done | bytes 1572896 | tf_op jit(solution)/shard_map/ppermute | solution.py:45
  129.8 9.6 fusion.28
  146.8 43.1 %spread_0.1 = f32[32,8,128]{2,1,0:T(8,128)} custom-call(f32[8,128]{1,0:T(8,128)} %bitcast_convert_fusion.tile_ref), custom_call_target="tpu_custom_call" | custom-call | tf_op jit(solution)/shard_map/spread_0/pallas_call | solution.py:247
  208.2 10.8 collective-permute-done.3
  298.7 13.6 fusion.154
  380.3 73.2 %all-gather.34.cloned.1.call-done = bf16[1,1,1024,4096]{3,2,1,0:T(8,128)(2,1)} async-done(((bf16[1,1,32,4096]{3,2,1,0:T(8,128)(2,1)}), bf16[1,1,1024,4096]{3,2,1,0:T(8,128)(2,1)}) %all-gather.34.cloned.1.call-update) | async-done | bytes 8388624 | tf_op jit(solution)/shard_map/all_gather | solution.py:643
  453.5 19.9 %multiply_convert_fusion.2 = (bf16[384,4096]{1,0:T(8,128)(2,1)}, f32[384,4096]{1,0:T(8,128)}, f32[384,4096]{1,0:T(8,128)}) fusion(bf16[384,1024]{1,0:T(8,128)(2,1)S(1)} %add_convert_fusion.3, bf16[1,1,1024,4096]{3,2,1,0:T(8,128)(2,1)} %all-gather.34.cloned.1.call-done), kind=kOutput, calls=%fused_computation.41 | convolution fusion | flops 3323461632 | bytes 24903680 | tf_op jit(solution)/shard_map/dot_general | solution.py:29
  473.4 59.4 %all-gather.36.cloned.1.call-done = bf16[1,1,1024,4096]{3,2,1,0:T(8,128)(2,1)} async-done(((bf16[1,1,32,4096]{3,2,1,0:T(8,128)(2,1)}), bf16[1,1,1024,4096]{3,2,1,0:T(8,128)(2,1)}) %all-gather.36.cloned.1.call-update) | async-done | bytes 8388624 | tf_op jit(solution)/shard_map/all_gather | solution.py:643
  544.0 9.2 collective-permute-done.11
  564.7 8.9 collective-permute-done.12
  610.4 27.2 %all-gather.20.cloned.1.call-done = bf16[1024,1024]{1,0:T(8,128)(2,1)} async-done(((bf16[32,1024]{1,0:T(8,128)(2,1)}), bf16[1024,1024]{1,0:T(8,128)(2,1)}) %all-gather.20.cloned.1.call-update) | async-done | bytes 2097168 | tf_op jit(solution)/shard_map/all_gather | solution.py:644
  679.2 10.1 all_gather.43
  703.1 9.1 fusion.161
  719.3 8.4 convolution_add_fusion
  731.6 10.3 fusion.160
  745.3 12.8 convolution_add_fusion.1
  798.7 10.9 collective-permute-done.16
  815.2 11.0 add_convert_fusion
  873.4 8.0 all-to-all-done.7
  999.6 10.2 collective-permute-done.42
  1082.8 11.6 dynamic-slice_convert_fusion.1
  1131.7 50.3 %collective-permute-done.23 = bf16[6,256,1024]{2,1,0:T(8,128)(2,1)S(1)} collective-permute-done((bf16[6,256,1024]{2,1,0:T(8,128)(2,1)}, bf16[6,256,1024]{2,1,0:T(8,128)(2,1)S(1)}, u32[]{:S(2)}, u32[]{:S(2)}) %collective-permute-start.23) | collective-permute-done | bytes 3145760 | tf_op jit(solution)/shard_map/ppermute | solution.py:45
  1188.0 11.0 collective-permute-done.28
  1214.8 11.3 collective-permute-done.20
  1226.2 12.2 collective-permute-done.24
  1240.1 9.0 collective-permute-done.29
  1253.9 30.4 %collective-permute-done.21 = bf16[3,32,1024]{2,1,0:T(8,128)(2,1)S(1)} collective-permute-done((bf16[3,32,1024]{2,1,0:T(8,128)(2,1)S(1)}, bf16[3,32,1024]{2,1,0:T(8,128)(2,1)S(1)}, u32[]{:S(2)}, u32[]{:S(2)}) %collective-permute-start.21) | collective-permute-done | bytes 196640 | tf_op jit(solution)/shard_map/ppermute | solution.py:45
  1288.1 23.8 %collective-permute-done.26 = bf16[6,32,1024]{2,1,0:T(8,128)(2,1)S(1)} collective-permute-done((bf16[6,32,1024]{2,1,0:T(8,128)(2,1)S(1)}, bf16[6,32,1024]{2,1,0:T(8,128)(2,1)S(1)}, u32[]{:S(2)}, u32[]{:S(2)}) %collective-permute-start.26) | collective-permute-done | bytes 393248 | tf_op jit(solution)/shard_map/ppermute | solution.py:45
  1328.3 12.1 spread_1.1
  (1021 shorter events, 703.9 us)
Async XLA Ops:
  7.2 122.6 %all-gather.22.cloned.1.call-start = ((), (), s32[]{:S(2)}) async-start(), calls=%async_computation.13 | async-start | bytes 4718592 | tf_op jit(solution)/shard_map/all_gather | solution.py:627
  10.2 319.6 %all-gather.24.cloned.1.call-start = ((), (), s32[]{:S(2)}) async-start(), calls=%async_computation.14 | async-start | bytes 2162688 | tf_op jit(solution)/shard_map/all_gather | solution.py:641
  11.1 326.1 %all-gather.28.cloned.1.call-start = ((), (), s32[]{:S(2)}) async-start(), calls=%async_computation.16 | async-start | bytes 2162688 | tf_op jit(solution)/shard_map/all_gather | solution.py:641
  11.8 334.5 %all-gather.30.cloned.1.call-start = ((), (), s32[]{:S(2)}) async-start(), calls=%async_computation.17 | async-start | bytes 2162688 | tf_op jit(solution)/shard_map/all_gather | solution.py:641
  12.4 335.9 %all-gather.26.cloned.1.call-start = ((), (), s32[]{:S(2)}) async-start(), calls=%async_computation.15 | async-start | bytes 2162688 | tf_op jit(solution)/shard_map/all_gather | solution.py:641
  13.0 360.3 %all-gather.32.cloned.1.call-start = ((), (), s32[]{:S(2)}) async-start(), calls=%async_computation.18 | async-start | bytes 2162688 | tf_op jit(solution)/shard_map/all_gather | solution.py:641
  13.6 440.0 %all-gather.34.cloned.1.call-start = ((), (), s32[]{:S(2)}) async-start(), calls=%async_computation.19 | async-start | bytes 8650752 | tf_op jit(solution)/shard_map/all_gather | solution.py:643
  14.5 518.3 %all-gather.36.cloned.1.call-start = ((), (), s32[]{:S(2)}) async-start(), calls=%async_computation.20 | async-start | bytes 8650752 | tf_op jit(solution)/shard_map/all_gather | solution.py:643
  15.3 564.7 %all-gather.38.cloned.1.call-start = ((), (), s32[]{:S(2)}) async-start(), calls=%async_computation.21 | async-start | bytes 4718592 | tf_op jit(solution)/shard_map/all_gather | solution.py:645
  16.0 621.6 %all-gather.20.cloned.1.call-start = ((), (), s32[]{:S(2)}) async-start(), calls=%async_computation.12 | async-start | bytes 2162688 | tf_op jit(solution)/shard_map/all_gather | solution.py:644
  86.2 39.5 %collective-permute-start.7 = (bf16[3,2,2,2,32,1024]{5,4,3,2,1,0:T(8,128)(2,1)S(1)}, bf16[3,2,2,2,32,1024]{5,4,3,2,1,0:T(8,128)(2,1)}, u32[]{:S(2)}, u32[]{:S(2)}) collective-permute-start(bf16[3,2,2,2,32,1024]{5,4,3,2,1,0:T(8,128)(2,1)S(1)} %pad_maximum_fusion.10), channel_id=1, source_target_pairs={{0,16},{8,24},{16,0},{24,8},{1,17},{9,25},{17,1},{25,9},{2,18},{10... | collective-permute-start | bytes 4718600 | tf_op jit(solution)/shard_map/ppermute | solution.py:45
  129.8 73.7 %collective-permute-start.8 = (bf16[3,2,2,2,2,32,1024]{6,5,4,3,2,1,0:T(8,128)(2,1)}, bf16[3,2,2,2,2,32,1024]{6,5,4,3,2,1,0:T(8,128)(2,1)}, u32[]{:S(2)}, u32[]{:S(2)}) collective-permute-start(bf16[3,2,2,2,2,32,1024]{6,5,4,3,2,1,0:T(8,128)(2,1)} %pad_maximum_fusion.4), channel_id=1, source_target_pairs={{0,1},{1,0},{2,3},{3,2},{4,5},{5,4},{6,7},{7,6},{8,9},{9,8},{10,11... | collective-permute-start | bytes 9437192 | tf_op jit(solution)/shard_map/ppermute | solution.py:45
  142.1 54.3 %collective-permute-start.2 = (f32[2,384,512]{2,1,0:T(8,128)}, f32[2,384,512]{2,1,0:T(8,128)}, u32[]{:S(2)}, u32[]{:S(2)}) collective-permute-start(f32[2,384,512]{2,1,0:T(8,128)} %bitcast.9), channel_id=1, source_target_pairs={{0,16},{8,24},{16,0},{24,8},{1,17},{9,25},{17,1},{25,9},{2,18},{10... | collective-permute-start | bytes 4718600 | tf_op jit(solution)/shard_map/ppermute | solution.py:45
  144.1 56.6 %collective-permute-start = (f32[2,384,512]{2,1,0:T(8,128)}, f32[2,384,512]{2,1,0:T(8,128)}, u32[]{:S(2)}, u32[]{:S(2)}) collective-permute-start(f32[2,384,512]{2,1,0:T(8,128)} %slice_bitcast_fusion.2), channel_id=1, source_target_pairs={{0,8},{8,0},{16,24},{24,16},{1,9},{9,1},{17,25},{25,17},{2,10},{10... | collective-permute-start | bytes 4718600 | tf_op jit(solution)/shard_map/ppermute | solution.py:45
  742.0 45.6 %collective-permute-start.15 = (f32[2,384,512]{2,1,0:T(8,128)}, f32[2,384,512]{2,1,0:T(8,128)}, u32[]{:S(2)}, u32[]{:S(2)}) collective-permute-start(f32[2,384,512]{2,1,0:T(8,128)} %bitcast.96), channel_id=1, source_target_pairs={{0,16},{8,24},{16,0},{24,8},{1,17},{9,25},{17,1},{25,9},{2,18},{10... | collective-permute-start | bytes 4718600 | tf_op jit(solution)/shard_map/ppermute | solution.py:45
  744.6 46.4 %collective-permute-start.13 = (f32[2,384,512]{2,1,0:T(8,128)}, f32[2,384,512]{2,1,0:T(8,128)}, u32[]{:S(2)}, u32[]{:S(2)}) collective-permute-start(f32[2,384,512]{2,1,0:T(8,128)} %slice_bitcast_fusion), channel_id=1, source_target_pairs={{0,8},{8,0},{16,24},{24,16},{1,9},{9,1},{17,25},{25,17},{2,10},{10... | collective-permute-start | bytes 4718600 | tf_op jit(solution)/shard_map/ppermute | solution.py:45
  797.4 200.6 %collective-permute-start.40 = (bf16[4,2,64,1024]{3,2,0,1:T(8,128)(2,1)}, bf16[4,2,64,1024]{3,2,0,1:T(8,128)(2,1)}, u32[]{:S(2)}, u32[]{:S(2)}) collective-permute-start(bf16[4,2,64,1024]{3,2,0,1:T(8,128)(2,1)} %fusion.167), channel_id=1, source_target_pairs={{0,2},{1,3},{2,0},{3,1},{4,6},{5,7},{6,4},{7,5},{8,10},{9,11},{10,... | collective-permute-start | bytes 3145736 | tf_op jit(solution)/shard_map/ppermute | solution.py:45
  860.2 222.6 %collective-permute-start.27 = (bf16[2,512,4096]{2,1,0:T(8,128)(2,1)}, bf16[2,512,4096]{2,1,0:T(8,128)(2,1)}, u32[]{:S(2)}, u32[]{:S(2)}) collective-permute-start(bf16[2,512,4096]{2,1,0:T(8,128)(2,1)} %pad_maximum_fusion), channel_id=1, source_target_pairs={{0,1},{1,0},{2,3},{3,2},{4,5},{5,4},{6,7},{7,6},{8,9},{9,8},{10,11... | collective-permute-start | bytes 25165832 | tf_op jit(solution)/shard_map/ppermute | solution.py:45
  904.8 163.6 %collective-permute-start.22 = (bf16[6,512,1024]{2,1,0:T(8,128)(2,1)}, bf16[6,512,1024]{2,1,0:T(8,128)(2,1)}, u32[]{:S(2)}, u32[]{:S(2)}) collective-permute-start(bf16[6,512,1024]{2,1,0:T(8,128)(2,1)} %fusion.125), channel_id=1, source_target_pairs={{0,1},{1,0},{2,3},{3,2},{4,5},{5,4},{6,7},{7,6},{8,9},{9,8},{10,11... | collective-permute-start | bytes 18874376 | tf_op jit(solution)/shard_map/ppermute | solution.py:45
  992.4 61.8 %collective-permute-start.17 = (bf16[3,512,1024]{2,1,0:T(8,128)(2,1)}, bf16[3,512,1024]{2,1,0:T(8,128)(2,1)}, u32[]{:S(2)}, u32[]{:S(2)}) collective-permute-start(bf16[3,512,1024]{2,1,0:T(8,128)(2,1)} %pad_maximum_fusion.6), channel_id=1, source_target_pairs={{0,1},{1,0},{2,3},{3,2},{4,5},{5,4},{6,7},{7,6},{8,9},{9,8},{10,11... | collective-permute-start | bytes 9437192 | tf_op jit(solution)/shard_map/ppermute | solution.py:45
  1040.1 166.6 %collective-permute-start.41 = (bf16[4,64,1024]{2,1,0:T(8,128)(2,1)}, bf16[4,64,1024]{2,1,0:T(8,128)(2,1)}, u32[]{:S(2)}, u32[]{:S(2)}) collective-permute-start(bf16[4,64,1024]{2,1,0:T(8,128)(2,1)} %fusion.215), channel_id=1, source_target_pairs={{0,4},{1,5},{2,6},{3,7},{4,0},{5,1},{6,2},{7,3},{8,12},{9,13},{10,... | collective-permute-start | bytes 1572872 | tf_op jit(solution)/shard_map/ppermute | solution.py:45
  1044.4 158.5 %collective-permute-start.45 = (f32[8,1024]{1,0:T(8,128)S(1)}, f32[8,1024]{1,0:T(8,128)S(1)}, u32[]{:S(2)}, u32[]{:S(2)}) collective-permute-start(f32[8,1024]{1,0:T(8,128)S(1)} %add.913), channel_id=1, source_target_pairs={{0,2},{1,3},{2,0},{3,1},{4,6},{5,7},{6,4},{7,5},{8,10},{9,11},{10,... | collective-permute-start | bytes 98312 | tf_op jit(solution)/shard_map/ppermute | solution.py:45
  1064.1 49.2 %collective-permute-start.18 = (bf16[3,256,1024]{2,1,0:T(8,128)(2,1)}, bf16[3,256,1024]{2,1,0:T(8,128)(2,1)}, u32[]{:S(2)}, u32[]{:S(2)}) collective-permute-start(bf16[3,256,1024]{2,1,0:T(8,128)(2,1)} %pad_maximum_fusion.14), channel_id=1, source_target_pairs={{0,8},{8,0},{16,24},{24,16},{1,9},{9,1},{17,25},{25,17},{2,10},{10... | collective-permute-start | bytes 4718600 | tf_op jit(solution)/shard_map/ppermute | solution.py:45
  1105.9 93.1 %collective-permute-start.28 = (bf16[2,256,4096]{2,1,0:T(8,128)(2,1)}, bf16[2,256,4096]{2,1,0:T(8,128)(2,1)}, u32[]{:S(2)}, u32[]{:S(2)}) collective-permute-start(bf16[2,256,4096]{2,1,0:T(8,128)(2,1)} %pad_maximum_fusion.3), channel_id=1, source_target_pairs={{0,8},{8,0},{16,24},{24,16},{1,9},{9,1},{17,25},{25,17},{2,10},{10... | collective-permute-start | bytes 12582920 | tf_op jit(solution)/shard_map/ppermute | solution.py:45
  1111.6 70.4 %collective-permute-start.23 = (bf16[6,256,1024]{2,1,0:T(8,128)(2,1)}, bf16[6,256,1024]{2,1,0:T(8,128)(2,1)S(1)}, u32[]{:S(2)}, u32[]{:S(2)}) collective-permute-start(bf16[6,256,1024]{2,1,0:T(8,128)(2,1)} %fusion.203), channel_id=1, source_target_pairs={{0,16},{8,24},{16,0},{24,8},{1,17},{9,25},{17,1},{25,9},{2,18},{10... | collective-permute-start | bytes 9437192 | tf_op jit(solution)/shard_map/ppermute | solution.py:45
  1113.3 97.8 %collective-permute-start.37 = (bf16[4,2,64,1024]{3,2,1,0:T(8,128)(2,1)}, bf16[4,2,64,1024]{3,2,1,0:T(8,128)(2,1)}, u32[]{:S(2)}, u32[]{:S(2)}) collective-permute-start(bf16[4,2,64,1024]{3,2,1,0:T(8,128)(2,1)} %fusion.166), channel_id=1, source_target_pairs={{0,2},{1,3},{2,0},{3,1},{4,6},{5,7},{6,4},{7,5},{8,10},{9,11},{10,... | collective-permute-start | bytes 3145736 | tf_op jit(solution)/shard_map/ppermute | solution.py:45
  1202.1 46.9 %collective-permute-start.29 = (bf16[2,2,2,32,4096]{4,3,0,1,2:T(8,128)(2,1)S(1)}, bf16[2,2,2,32,4096]{4,3,0,1,2:T(8,128)(2,1)S(1)}, u32[]{:S(2)}, u32[]{:S(2)}) collective-permute-start(bf16[2,2,2,32,4096]{4,3,0,1,2:T(8,128)(2,1)S(1)} %fusion.60), channel_id=1, source_target_pairs={{0,16},{8,24},{16,0},{24,8},{1,17},{9,25},{17,1},{25,9},{2,18},{10... | collective-permute-start | bytes 6291464 | tf_op jit(solution)/shard_map/ppermute | solution.py:45
  1203.0 35.4 %collective-permute-start.24 = (bf16[6,2,2,32,1024]{4,3,0,1,2:T(8,128)(2,1)S(1)}, bf16[6,2,2,32,1024]{4,3,0,1,2:T(8,128)(2,1)S(1)}, u32[]{:S(2)}, u32[]{:S(2)}) collective-permute-start(bf16[6,2,2,32,1024]{4,3,0,1,2:T(8,128)(2,1)S(1)} %fusion.80), channel_id=1, source_target_pairs={{0,8},{8,0},{16,24},{24,16},{1,9},{9,1},{17,25},{25,17},{2,10},{10... | collective-permute-start | bytes 4718600 | tf_op jit(solution)/shard_map/ppermute | solution.py:45
  1212.8 39.8 %collective-permute-start.38 = (bf16[4,64,1024]{2,1,0:T(8,128)(2,1)S(1)}, bf16[4,64,1024]{2,1,0:T(8,128)(2,1)S(1)}, u32[]{:S(2)}, u32[]{:S(2)}) collective-permute-start(bf16[4,64,1024]{2,1,0:T(8,128)(2,1)S(1)} %fusion.214), channel_id=1, source_target_pairs={{0,4},{1,5},{2,6},{3,7},{4,0},{5,1},{6,2},{7,3},{8,12},{9,13},{10,... | collective-permute-start | bytes 1572872 | tf_op jit(solution)/shard_map/ppermute | solution.py:45
  1239.3 45.1 %collective-permute-start.25 = (bf16[6,2,32,1024]{3,2,0,1:T(8,128)(2,1)S(1)}, bf16[6,2,32,1024]{3,2,0,1:T(8,128)(2,1)S(1)}, u32[]{:S(2)}, u32[]{:S(2)}) collective-permute-start(bf16[6,2,32,1024]{3,2,0,1:T(8,128)(2,1)S(1)} %fusion.193), channel_id=1, source_target_pairs={{0,2},{1,3},{2,0},{3,1},{4,6},{5,7},{6,4},{7,5},{8,10},{9,11},{10,... | collective-permute-start | bytes 2359304 | tf_op jit(solution)/shard_map/ppermute | solution.py:45
  1249.9 34.8 %collective-permute-start.30 = (bf16[2,2,32,4096]{3,2,0,1:T(8,128)(2,1)S(1)}, bf16[2,2,32,4096]{3,2,0,1:T(8,128)(2,1)S(1)}, u32[]{:S(2)}, u32[]{:S(2)}) collective-permute-start(bf16[2,2,32,4096]{3,2,0,1:T(8,128)(2,1)S(1)} %fusion.165), channel_id=1, source_target_pairs={{0,2},{1,3},{2,0},{3,1},{4,6},{5,7},{6,4},{7,5},{8,10},{9,11},{10,... | collective-permute-start | bytes 3145736 | tf_op jit(solution)/shard_map/ppermute | solution.py:45
  1285.1 36.9 %collective-permute-start.31 = (bf16[2,32,4096]{2,1,0:T(8,128)(2,1)S(1)}, bf16[2,32,4096]{2,1,0:T(8,128)(2,1)S(1)}, u32[]{:S(2)}, u32[]{:S(2)}) collective-permute-start(bf16[2,32,4096]{2,1,0:T(8,128)(2,1)S(1)} %fusion.213), channel_id=1, source_target_pairs={{0,4},{1,5},{2,6},{3,7},{4,0},{5,1},{6,2},{7,3},{8,12},{9,13},{10,... | collective-permute-start | bytes 1572872 | tf_op jit(solution)/shard_map/ppermute | solution.py:45
  (268 other events, 4174.0 us)
Sparse Core Ops, SparseCore 0:
  10.3 58.0 all-gather.21
  72.0 57.6 all-gather.23
  133.3 60.0 all-gather.27
  196.7 57.5 all-gather.29
  257.8 55.8 all-gather.25
  317.1 56.0 all-gather.31
  376.8 76.6 all-gather.33
  457.1 75.6 all-gather.35
  535.0 44.2 all-gather.37
  582.1 55.4 all-gather.19
